TPU v7x, 32 devices: a whole 2x2x4 slice. The times are simulated.
32 devices in a mesh: dp: 4 (over z), neg: 8 (over y, x, core).
Axes of the slice: x: 2, y: 2, z: 4, core: 2. Of those that a mesh axis runs over, the one named last changes fastest.
Arguments:
- query_emb: bfloat16 [128, 32, 128], P(('dp', 'neg')), may hold values from -6 to 6
- positive: int32 [128], P(('dp', 'neg')), may hold values from 0 to 31
- passage_emb: bfloat16 [32, 512, 128], P(('dp', 'neg')), may hold values from -6 to 6
- lengths: int32 [32], P(('dp', 'neg')), may hold values from 256 to 512
- residual: bfloat16 [16384, 1024], P(('dp', 'neg')), may hold values from -6 to 6
- context: bfloat16 [16384, 1024], P(('dp', 'neg')), may hold values from -6 to 6
- out_proj: bfloat16 [1024, 1024], replicated, may hold values from -0.1875 to 0.1875
- norm_gain: float32 [1024], replicated, may hold values from 0.5 to 1.5
- colbert_proj: bfloat16 [1024, 128], replicated, may hold values from -0.1875 to 0.1875
Outputs:
- loss: float32 [], replicated
- query_grad: float32 [128, 32, 128], P(('dp', 'neg'))
- residual_grad: bfloat16 [16384, 1024], P(('dp', 'neg'))
- context_grad: bfloat16 [16384, 1024], P(('dp', 'neg'))
- out_proj_grad: float32 [1024, 1024], replicated
- colbert_grad: float32 [1024, 128], replicated
- gain_grad: float32 [1024], replicated
Inputs may be any that keep to these rules, and one draw needn't show every extreme that they name: A passage's first lengths[p] token slots are real, the rest padding.
All inputs are finite; a program needn't handle non-finite values.
Results may differ from a plain program's by a relative error of at most 0.0065.
Values may be sent and summed in bfloat16 or wider, within the bound.
A program may use at most 64 MiB of HBM per device.

v0:
```python
import functools

import jax
import jax.numpy as jnp
from jax import lax
from jax.experimental import pallas as pl
from jax.experimental.pallas import tpu as pltpu
from jax.sharding import PartitionSpec as P

MESH = pl.DeviceIdType.MESH
VMEM = pl.BlockSpec(memory_space=pltpu.VMEM)
LANES = 128
LOW = -1e30


def place(axis, size, step):
    there = lax.rem(lax.axis_index(axis) + step + size, size)
    if axis == "dp":
        return (there, lax.axis_index("neg"))
    return (lax.axis_index("dp"), there)


def greet(sizes):
    barrier = pltpu.get_barrier_semaphore()
    for axis, size in sizes:

        def tell(k, carry):
            pl.semaphore_signal(
                barrier, inc=1, device_id=place(axis, size, k), device_id_type=MESH
            )
            return carry

        lax.fori_loop(1, size, tell, 0)
    pl.semaphore_wait(barrier, sum(size - 1 for _, size in sizes))


def remote(src, dst, send, recv, device):
    return pltpu.make_async_remote_copy(
        src_ref=src, dst_ref=dst, send_sem=send, recv_sem=recv, device_id=device, device_id_type=MESH
    )


def each(size, act):
    def turn(k, carry):
        act(k)
        return carry

    lax.fori_loop(1, size, turn, 0)


def gather_kernel(sizes, plan, *refs):
    count = len(plan)
    ins, outs, sems = refs[:count], refs[count : 2 * count], refs[2 * count :]
    greet([(axis, sizes[axis]) for axis in dict.fromkeys(plan)])
    for i, axis in enumerate(plan):
        me = lax.axis_index(axis)
        each(
            sizes[axis],
            lambda k: remote(
                ins[i], outs[i].at[me], sems[2 * i].at[k], sems[2 * i + 1].at[k], place(axis, sizes[axis], k)
            ).start(),
        )
    for i, axis in enumerate(plan):
        outs[i][lax.axis_index(axis)] = ins[i][...]
    for i, axis in enumerate(plan):
        size = sizes[axis]
        me = lax.axis_index(axis)

        def finish(k):
            slot = lax.rem(me - k + size, size)
            copy = remote(
                ins[i], outs[i].at[slot], sems[2 * i].at[k], sems[2 * i + 1].at[k], place(axis, size, k)
            )
            copy.wait_recv()
            copy.wait_send()

        each(size, finish)


def gather(sizes, ident, pairs):
    plan = tuple(axis for _, axis in pairs)
    arrays = [array for array, _ in pairs]
    sems = []
    for axis in plan:
        sems += [pltpu.SemaphoreType.DMA((sizes[axis],))] * 2
    return pl.pallas_call(
        functools.partial(gather_kernel, sizes, plan),
        out_shape=[
            jax.ShapeDtypeStruct((sizes[axis],) + array.shape, array.dtype) for array, axis in pairs
        ],
        in_specs=[VMEM] * len(plan),
        out_specs=[VMEM] * len(plan),
        scratch_shapes=sems,
        compiler_params=pltpu.CompilerParams(collective_id=ident, has_side_effects=True),
    )(*arrays)


def scatter_kernel(sizes, plan, *refs):
    count = len(plan)
    ins, outs, rest = refs[:count], refs[count : 2 * count], refs[2 * count :]
    lands, sems = rest[:count], rest[count:]
    greet([(axis, sizes[axis]) for axis in plan])
    for i, axis in enumerate(plan):
        size = sizes[axis]
        me = lax.axis_index(axis)

        each(
            size,
            lambda k: remote(
                ins[i].at[lax.rem(me + k, size)],
                lands[i].at[k],
                sems[2 * i].at[k],
                sems[2 * i + 1].at[k],
                place(axis, size, k),
            ).start(),
        )
    for i, axis in enumerate(plan):
        size = sizes[axis]
        me = lax.axis_index(axis)

        def finish(k):
            copy = remote(
                ins[i].at[lax.rem(me + k, size)],
                lands[i].at[k],
                sems[2 * i].at[k],
                sems[2 * i + 1].at[k],
                place(axis, size, k),
            )
            copy.wait_recv()
            copy.wait_send()

        each(size, finish)
        total = ins[i][me].astype(jnp.float32)
        for k in range(1, size):
            total = total + lands[i][k].astype(jnp.float32)
        outs[i][...] = total.astype(outs[i].dtype)


def scatter(sizes, ident, triples):
    plan = tuple(axis for _, axis, _ in triples)
    sems, lands = [], []
    for array, axis, _ in triples:
        lands.append(pltpu.VMEM(array.shape, array.dtype))
        sems += [pltpu.SemaphoreType.DMA((sizes[axis],))] * 2
    return pl.pallas_call(
        functools.partial(scatter_kernel, sizes, plan),
        out_shape=[jax.ShapeDtypeStruct(array.shape[1:], dtype) for array, _, dtype in triples],
        in_specs=[VMEM] * len(plan),
        out_specs=[VMEM] * len(plan),
        scratch_shapes=lands + sems,
        compiler_params=pltpu.CompilerParams(collective_id=ident, has_side_effects=True),
    )(*[array for array, _, _ in triples])


def total_kernel(dp, neg, part, gain, extra, out, small, pair_in, held, lands, mine, pair_small, all_small,
                 pair_s, pair_r, rs_s, rs_r, ag_s, ag_r, fw_s, fw_r, sm_s, sm_r, sp_s, sp_r):
    groups = neg // 2
    n = dp * groups
    row, col = lax.axis_index("dp"), lax.axis_index("neg")
    core = lax.rem(col, 2)
    other = 1 - core
    me = row * groups + col // 2
    partner = (row, col + 1 - 2 * core)

    def at(k):
        return lax.rem(me + k + n, n)

    def device(k):
        t = at(k)
        return (t // groups, lax.rem(t, groups) * 2 + core)

    barrier = pltpu.get_barrier_semaphore()
    pl.semaphore_signal(barrier, inc=1, device_id=partner, device_id_type=MESH)
    each(n, lambda k: pl.semaphore_signal(barrier, inc=1, device_id=device(k), device_id_type=MESH))
    pl.semaphore_wait(barrier, n)

    wide = gain.shape[1]
    mine[:, :wide] = gain[...]
    mine[:, wide:] = extra[...]

    def pair_copy(k):
        return remote(part.at[other, at(k)], pair_in.at[at(k)], pair_s.at[k], pair_r.at[k], partner)

    def rs_copy(k):
        return remote(held.at[at(k)], lands.at[k], rs_s.at[k], rs_r.at[k], device(k))

    each(n, lambda k: pair_copy(k).start())
    pair_copy(0).start()
    sp_copy = remote(mine, pair_small, sp_s, sp_r, partner)
    sp_copy.start()

    def join(k):
        pair_copy(k).wait_recv()
        t = at(k)
        held[t] = (part[core, t].astype(jnp.float32) + pair_in[t].astype(jnp.float32)).astype(held.dtype)

    def join_send(k):
        join(k)
        rs_copy(k).start()

    each(n, join_send)
    join(0)
    sp_copy.wait_recv()
    all_small[me] = mine[...] + pair_small[...]

    def sm_copy(k, slot):
        return remote(all_small.at[slot], all_small.at[slot], sm_s.at[k], sm_r.at[k], device(k))

    each(n, lambda k: sm_copy(k, me).start())

    def add(k, total):
        rs_copy(k).wait_recv()
        return total + lands[k].astype(jnp.float32)

    total = lax.fori_loop(1, n, add, held[me].astype(jnp.float32))
    out[core, me] = total.astype(out.dtype)

    def ag_copy(k, slot):
        return remote(out.at[core, slot], out.at[core, slot], ag_s.at[k], ag_r.at[k], device(k))

    def fw_copy(k, half):
        return remote(out.at[half, at(-k)], out.at[half, at(-k)], fw_s.at[k], fw_r.at[k], partner)

    each(n, lambda k: ag_copy(k, me).start())
    fw_copy(0, core).start()

    def pass_on(k):
        ag_copy(k, at(-k)).wait_recv()
        fw_copy(k, core).start()

    each(n, pass_on)
    each(n, lambda k: sm_copy(k, at(-k)).wait_recv())

    def add_small(k, so_far):
        return so_far + all_small[k]

    small[...] = lax.fori_loop(1, n, add_small, all_small[0])

    def drain(k):
        fw_copy(k, other).wait_recv()
        fw_copy(k, core).wait_send()
        pair_copy(k).wait_send()

    drain(0)
    sp_copy.wait_send()

    def drain_all(k):
        drain(k)
        rs_copy(k).wait_send()
        ag_copy(k, me).wait_send()
        sm_copy(k, me).wait_send()

    each(n, drain_all)


def total_sum(sizes, ident, part, gain, extra):
    dp, neg = sizes["dp"], sizes["neg"]
    n = dp * neg // 2
    rows, columns = part.shape
    part = part.reshape(2, n, rows // (2 * n), columns)
    piece = part.shape[1:]
    width = gain.shape[1] + extra.shape[1]
    dma = pltpu.SemaphoreType.DMA
    out, small = pl.pallas_call(
        functools.partial(total_kernel, dp, neg),
        out_shape=[
            jax.ShapeDtypeStruct(part.shape, part.dtype),
            jax.ShapeDtypeStruct((1, width), jnp.float32),
        ],
        in_specs=[VMEM] * 3,
        out_specs=[VMEM] * 2,
        scratch_shapes=[
            pltpu.VMEM(piece, part.dtype),
            pltpu.VMEM(piece, part.dtype),
            pltpu.VMEM(piece, part.dtype),
            pltpu.VMEM((1, width), jnp.float32),
            pltpu.VMEM((1, width), jnp.float32),
            pltpu.VMEM((n, 1, width), jnp.float32),
        ]
        + [dma((n,))] * 10
        + [dma] * 2,
        compiler_params=pltpu.CompilerParams(collective_id=ident, has_side_effects=True),
    )(part, gain, extra)
    return out.reshape(rows, columns), small


def select_tokens(rows, queries, per):
    token = lax.broadcasted_iota(jnp.int32, (rows, queries), 0)
    query = lax.broadcasted_iota(jnp.int32, (rows, queries), 1)
    return jnp.where(token // per == query, 1.0, 0.0)


def masked(passage, queries, length):
    scores = lax.dot_general(
        passage, queries, (((1,), (1,)), ((), ())), preferred_element_type=jnp.float32
    )
    position = lax.broadcasted_iota(jnp.int32, scores.shape, 0)
    return jnp.where(position < length, scores, LOW)


def forward_kernel(per, queries, passages, lengths, inner, similar):
    slots = passages.shape[0]
    tokens = queries.shape[0]
    inner[...] = jnp.zeros_like(inner)
    wide = tokens // 4 if tokens % 512 == 0 else tokens

    def one(p, carry):
        length = lengths[p, 0:1, 0:1]
        for start in range(0, tokens, wide):
            scores = masked(passages[p], queries[start : start + wide, :], length)
            highest = jnp.max(scores, axis=0, keepdims=True)
            lse = highest + jnp.log(jnp.sum(jnp.exp(scores - highest), axis=0, keepdims=True))
            inner[pl.ds(p, 1), start : start + wide] = lse
        return carry

    lax.fori_loop(0, slots, one, 0)
    chosen = select_tokens(tokens, similar.shape[1], per)
    summed = jnp.dot(
        inner[...], chosen, precision=lax.Precision.HIGHEST, preferred_element_type=jnp.float32
    )
    similar[...] = jnp.full_like(similar, LOW)
    for p in range(slots):
        shift = jnp.log(lengths[p, 0:1, 0:1].astype(jnp.float32)) * per
        similar[p : p + 1, :] = summed[p : p + 1, :] - shift


def backward_kernel(per, own, queries, passages, lengths, positives, inner, similar, everyone,
                    query_part, passage_part, loss_row, spread_coef, running):
    slots = passages.shape[0]
    tokens = queries.shape[0]
    neg = everyone.shape[0]
    here = lax.axis_index("neg")
    positive = positives[0]
    for s in range(1, neg):
        positive = positive + positives[s]
    positive = positive[0:1, :]
    highest = jnp.max(jnp.max(everyone[...], axis=0), axis=0, keepdims=True)
    row = lax.broadcasted_iota(jnp.int32, similar.shape, 0)
    exp_total = jnp.zeros(similar.shape, jnp.float32)
    score = jnp.zeros(similar.shape, jnp.float32)
    for s in range(neg):
        exp_total = exp_total + jnp.exp(everyone[s] - highest)
        score = score + jnp.where((row * neg + s == positive) & (row < slots), everyone[s], 0.0)
    log_total = highest + jnp.log(jnp.sum(exp_total, axis=0, keepdims=True))
    score = jnp.sum(score, axis=0, keepdims=True)
    lane = lax.broadcasted_iota(jnp.int32, log_total.shape, 1)
    mine = (lane >= here * own) & (lane < here * own + own)
    loss_row[...] = jnp.where(mine, log_total - score, 0.0)
    hit = jnp.where((row * neg + here == positive) & (row < slots), 1.0, 0.0)
    used = (row < slots) & (lax.broadcasted_iota(jnp.int32, similar.shape, 1) < tokens // per)
    coefficient = jnp.where(used, jnp.exp(similar[...] - log_total) - hit, 0.0)
    chosen = select_tokens(tokens, similar.shape[1], per)
    spread_coef[...] = lax.dot_general(
        coefficient, chosen, (((1,), (1,)), ((), ())),
        precision=lax.Precision.HIGHEST, preferred_element_type=jnp.float32,
    )
    running[...] = jnp.zeros_like(running)
    wide = tokens // 4 if tokens % 512 == 0 else tokens

    def one(p, carry):
        length = lengths[p, 0:1, 0:1]
        passage = passages[p]
        flipped = passage.astype(jnp.float32).T.astype(passage.dtype)
        total = jnp.zeros(passage.shape, jnp.float32)
        for start in range(0, tokens, wide):
            block = queries[start : start + wide, :]
            scores = masked(passage, block, length)
            spread = jnp.exp(scores - inner[pl.ds(p, 1), start : start + wide])
            weight = (spread * spread_coef[pl.ds(p, 1), start : start + wide]).astype(jnp.bfloat16)
            running[:, start : start + wide] += jnp.dot(
                flipped, weight, preferred_element_type=jnp.float32
            )
            total = total + jnp.dot(weight, block, preferred_element_type=jnp.float32)
        passage_part[p] = total.astype(passage_part.dtype)
        return carry

    lax.fori_loop(0, slots, one, 0)
    query_part[...] = running[...].T.astype(query_part.dtype)


def window_rows(resid_rows, context_rows, grad_rows, out_proj, norm_gain, colbert_proj):
    hidden = resid_rows.astype(jnp.float32) + jnp.dot(
        context_rows, out_proj, preferred_element_type=jnp.float32
    )
    row_mean = jnp.mean(hidden, axis=1, keepdims=True)
    centred = hidden - row_mean
    variance = jnp.mean(centred * centred, axis=1, keepdims=True)
    inv_std = 1.0 / jnp.sqrt(variance + 1e-05)
    normed = centred * inv_std
    scaled = (normed * norm_gain).astype(jnp.bfloat16)
    colbert_part = jnp.dot(scaled.T, grad_rows, preferred_element_type=jnp.float32)
    scaled_grad = jnp.dot(grad_rows, colbert_proj.T, preferred_element_type=jnp.float32)
    gain_part = jnp.sum(scaled_grad * normed, axis=0)
    gained = scaled_grad * norm_gain
    hidden_grad = (
        inv_std
        * (
            gained
            - jnp.mean(gained, axis=1, keepdims=True)
            - normed * jnp.mean(gained * normed, axis=1, keepdims=True)
        )
    ).astype(jnp.bfloat16)
    context_grad = jnp.dot(hidden_grad, out_proj.T, preferred_element_type=jnp.float32).astype(
        jnp.bfloat16
    )
    proj_part = jnp.dot(context_rows.T, hidden_grad, preferred_element_type=jnp.float32)
    return (hidden_grad, context_grad, proj_part, colbert_part, gain_part)


def body(sizes, query_emb, positive, passage_emb, lengths, residual, context, out_proj, norm_gain, colbert_proj):
    dp, neg = sizes["dp"], sizes["neg"]
    own, per, dim = query_emb.shape
    slots, plen = dp * passage_emb.shape[0], passage_emb.shape[1]
    group = own * neg
    tokens = group * per
    lanes = -(-group // LANES) * LANES
    rows = -(-slots // 8) * 8
    here = lax.axis_index("neg")
    pos_row = lax.dynamic_update_slice(jnp.zeros((8, lanes), jnp.int32), jnp.broadcast_to(positive, (8, own)), (0, here * own))
    len_row = jnp.broadcast_to(lengths, (8, LANES))
    queries, positives, passages, lens = gather(
        sizes,
        1,
        [
            (query_emb.reshape(own * per, dim), "neg"),
            (pos_row, "neg"),
            (passage_emb.reshape(plen, dim), "dp"),
            (len_row, "dp"),
        ],
    )
    queries = queries.reshape(tokens, dim)
    inner, similar = pl.pallas_call(
        functools.partial(forward_kernel, per),
        out_shape=[
            jax.ShapeDtypeStruct((rows, tokens), jnp.float32),
            jax.ShapeDtypeStruct((rows, lanes), jnp.float32),
        ],
        in_specs=[VMEM] * 3,
        out_specs=[VMEM] * 2,
    )(queries, passages, lens)
    (everyone,) = gather(sizes, 2, [(similar, "neg")])
    query_part, passage_part, loss_row = pl.pallas_call(
        functools.partial(backward_kernel, per, own),
        out_shape=[
            jax.ShapeDtypeStruct((tokens, dim), jnp.bfloat16),
            jax.ShapeDtypeStruct((slots, plen, dim), jnp.bfloat16),
            jax.ShapeDtypeStruct((1, lanes), jnp.float32),
        ],
        in_specs=[VMEM] * 7,
        out_specs=[VMEM] * 3,
        scratch_shapes=[pltpu.VMEM((rows, tokens), jnp.float32), pltpu.VMEM((dim, tokens), jnp.float32)],
    )(queries, passages, lens, positives, inner, similar, everyone)
    query_grad, emb_grad = scatter(
        sizes,
        3,
        [
            (query_part.reshape(neg, own * per, dim), "neg", jnp.float32),
            (passage_part, "dp", jnp.bfloat16),
        ],
    )
    residual_grad, context_grad, proj_part, colbert_part, gain_part = window_rows(
        residual, context, emb_grad, out_proj, norm_gain, colbert_proj
    )
    part = jnp.concatenate([proj_part.astype(jnp.bfloat16), colbert_part.astype(jnp.bfloat16)], axis=1)
    summed, small = total_sum(sizes, 4, part, gain_part[None, :], loss_row)
    width = norm_gain.shape[0]
    loss = jnp.sum(small[0, width:]) / (own * dp * neg)
    return (
        loss,
        query_grad.reshape(own, per, dim),
        residual_grad,
        context_grad,
        summed[:, :width].astype(jnp.float32),
        summed[:, width:].astype(jnp.float32),
        small[0, :width],
    )


def solution(mesh):
    sizes = {axis: mesh.shape[axis] for axis in ("dp", "neg")}
    split = ("dp", "neg")
    in_specs = (
        P(split, None, None),
        P(split),
        P(split, None, None),
        P(split),
        P(split, None),
        P(split, None),
        P(),
        P(),
        P(),
    )
    out_specs = (
        P(),
        P(split, None, None),
        P(split, None),
        P(split, None),
        P(),
        P(),
        P(),
    )
    return jax.shard_map(
        functools.partial(body, sizes), mesh=mesh, in_specs=in_specs, out_specs=out_specs, check_vma=False
    )
```

profile of v0, /device:TPU:29, one launch (start us, length us, event | category | flops | bytes accessed | tf_op | source)
XLA Modules:
  0.0 150.2 jit_solution(1795618992337318139)
XLA Ops:
  0.7 0.8 broadcast_in_dim.9
  2.3 0.6 broadcast_in_dim.10.refs_3_
  2.9 16.3 %shard_map.147 = (bf16[8,128,128]{2,1,0:T(8,128)(2,1)}, s32[8,8,128]{2,1,0:T(8,128)}, bf16[4,512,128]{2,1,0:T(8,128)(2,1)}, s32[4,8,128]{2,1,0:T(8,128)}) custom-call(bf16[128,128]{1,0:T(8,128)(2,1)} %bitcast.30, s32[8,128]{1,0:T(8,128)} %copy-done.6, bf16[512,128]{1,0:T(8,128)(2,1)} %bitcast.28, s32[8,128]{1,0:T(8,128)} %broadcast_in_dim.10.refs_3_), custom_call_target="tpu_custom_call" | custom-call | tf_op jit(solution)/shard_map/pallas_call | solution.py:86
  19.2 5.2 %shard_map.148 = (f32[8,1024]{1,0:T(8,128)}, f32[8,128]{1,0:T(8,128)}) custom-call(bf16[1024,128]{1,0:T(8,128)(2,1)} %bitcast.25, bf16[4,512,128]{2,1,0:T(8,128)(2,1)} %get-tuple-element.21.passages, s32[4,8,128]{2,1,0:T(8,128)} %get-tuple-element.22.lengths), custom_call_target="tpu_custom_call" | custom-call | tf_op jit(solution)/shard_map/pallas_call | solution.py:432
  24.4 7.2 %shard_map.149.everyone = f32[8,8,128]{2,1,0:T(8,128)} custom-call(f32[8,128]{1,0:T(8,128)} %get-tuple-element.25.refs_0_.similar), custom_call_target="tpu_custom_call" | custom-call | tf_op jit(solution)/shard_map/pallas_call | solution.py:86
  31.6 7.9 %shard_map.150 = (bf16[1024,128]{1,0:T(8,128)(2,1)}, bf16[4,512,128]{2,1,0:T(8,128)(2,1)}, f32[1,128]{1,0:T(1,128)}) custom-call(bf16[1024,128]{1,0:T(8,128)(2,1)} %bitcast.26, bf16[4,512,128]{2,1,0:T(8,128)(2,1)} %get-tuple-element.21.passages, s32[4,8,128]{2,1,0:T(8,128)} %get-tuple-element.22.lengths, s32[8,8,128]{2,1,0:T(8,128)} %get-tuple-element.23.positives, ...), custom_call_target="tpu_custom_call" | custom-call | tf_op jit(solution)/shard_map/pallas_call | solution.py:442
  39.5 16.0 %shard_map.151 = (f32[128,128]{1,0:T(8,128)}, bf16[512,128]{1,0:T(8,128)(2,1)}) custom-call(bf16[8,128,128]{2,1,0:T(8,128)(2,1)} %bitcast.27, bf16[4,512,128]{2,1,0:T(8,128)(2,1)} %get-tuple-element.27.refs_1_), custom_call_target="tpu_custom_call" | custom-call | tf_op jit(solution)/shard_map/pallas_call | solution.py:145
  55.6 2.6 %fusion.3 = (f32[512]{0:T(512)S(1)}, f32[512,1024]{1,0:T(8,128)S(1)}) fusion(bf16[512,1024]{1,0:T(8,128)(2,1)} %param.14, bf16[1024,1024]{1,0:T(8,128)(2,1)S(1)} %copy-done, bf16[512,1024]{1,0:T(8,128)(2,1)S(1)} %copy-done.8), kind=kOutput, calls=%fused_computation.22 | convolution fusion | flops 1075314176 | bytes 6293504 | tf_op jit(solution)/shard_map/dot_general | solution.py:382
  58.2 0.3 multiply_reduce_fusion.2
  58.6 0.5 copy-done.2
  59.2 1.4 multiply_reduce_fusion
  60.6 0.6 multiply_convert_fusion.1
  61.2 0.6 copy-done.9
  61.8 1.3 convert_bitcast_fusion
  63.1 0.5 convolution_convert_fusion.1
  63.6 1.6 %pad_maximum_fusion = bf16[1024,1152]{0,1:T(8,128)(2,1)} fusion(bf16[1024,128]{0,1:T(8,128)(2,1)S(1)} %convolution_convert_fusion.1, bf16[1024,1024]{0,1:T(8,128)(2,1)S(1)} %convert_bitcast_fusion), kind=kLoop, calls=%fused_computation | loop fusion | flops 4718592 | bytes 4718592 | tf_op jit(solution)/shard_map/concatenate | solution.py:464
  65.2 4.3 %copy.16 = bf16[1024,1152]{1,0:T(8,128)(2,1)} copy(bf16[1024,1152]{0,1:T(8,128)(2,1)} %pad_maximum_fusion) | data formatting | bytes 4718592 | tf_op jit(solution)/shard_map/concatenate | solution.py:464
  69.6 68.9 %shard_map.152 = (bf16[2,16,32,1152]{3,2,1,0:T(8,128)(2,1)}, f32[1,1152]{1,0:T(1,128)}) custom-call(bf16[2,16,32,1152]{3,2,1,0:T(8,128)(2,1)} %bitcast.22, f32[1,1024]{1,0:T(1,128)} %bitcast.31, f32[1,128]{1,0:T(1,128)} %get-tuple-element.29.extra), custom_call_target="tpu_custom_call" | custom-call | tf_op jit(solution)/shard_map/pallas_call | solution.py:264
  138.5 4.1 %slice_convert_fusion = f32[1024,1024]{1,0:T(8,128)} fusion(bf16[1024,1152]{1,0:T(8,128)(2,1)} %bitcast.23), kind=kLoop, calls=%fused_computation.1 | loop fusion | flops 1048576 | bytes 6291456 | tf_op jit(solution)/shard_map/convert_element_type | solution.py:473
  142.5 1.8 %slice_convert_fusion.1 = f32[1024,128]{1,0:T(8,128)} fusion(bf16[1024,1152]{1,0:T(8,128)(2,1)} %bitcast.24), kind=kLoop, calls=%fused_computation.16 | loop fusion | flops 131072 | bytes 786432 | tf_op jit(solution)/shard_map/convert_element_type | solution.py:474
  144.3 0.6 slice.15
  144.9 0.6 slice_reduce_fusion
  146.2 2.3 %convolution_convert_fusion = bf16[512,1024]{1,0:T(8,128)(2,1)} fusion(bf16[512,1024]{1,0:T(8,128)(2,1)S(1)} %multiply_convert_fusion.1, bf16[1024,1024]{1,0:T(8,128)(2,1)S(1)} %copy-done), kind=kOutput, calls=%fused_computation.11 | convolution fusion | flops 1074266112 | bytes 4194304 | tf_op jit(solution)/shard_map/dot_general | solution.py:403
  148.5 0.6 copy.20
  (23 shorter events, 0.3 us)
Async XLA Ops:
  0.6 55.0 %copy-start = (bf16[1024,1024]{1,0:T(8,128)(2,1)S(1)}, bf16[1024,1024]{1,0:T(8,128)(2,1)}, u32[]{:S(2)}) copy-start(bf16[1024,1024]{1,0:T(8,128)(2,1)} %param.15) | copy-start | bytes 6291460
  0.6 55.0 %copy-start.8 = (bf16[512,1024]{1,0:T(8,128)(2,1)S(1)}, bf16[512,1024]{1,0:T(8,128)(2,1)}, u32[]{:S(2)}) copy-start(bf16[512,1024]{1,0:T(8,128)(2,1)} %param.13) | copy-start | bytes 3145732
  1.6 1.3 copy-start.6
  58.2 0.9 copy-start.2
  58.2 1.0 copy-start.3
  58.2 1.0 copy-start.5
  60.6 1.2 copy-start.9
  61.8 84.4 %copy-start.1 = (bf16[512,1024]{1,0:T(8,128)(2,1)}, bf16[512,1024]{1,0:T(8,128)(2,1)S(1)}, u32[]{:S(2)}) copy-start(bf16[512,1024]{1,0:T(8,128)(2,1)S(1)} %multiply_convert_fusion.1) | copy-start | bytes 3145732
  138.5 5.9 %copy-start.7 = (f32[1,1152]{1,0:T(1,128)S(1)}, f32[1,1152]{1,0:T(1,128)}, u32[]{:S(2)}) copy-start(f32[1,1152]{1,0:T(1,128)} %get-tuple-element.30) | copy-start | bytes 13828
  146.2 2.3 %copy-start.4 = (f32[128,128]{1,0:T(8,128)S(1)}, f32[128,128]{1,0:T(8,128)}, u32[]{:S(2)}) copy-start(f32[128,128]{1,0:T(8,128)} %get-tuple-element.31) | copy-start | bytes 196612
where the time goes:
time: 151 us; the launch traced here: 150 us
  Pallas kernels  122 us (81%)
  other arithmetic  9.03 us (6%)
  local copies, waits for them, and re-layouts  8.38 us (6%)
  matrix products  8 us (5%)
  between operations  3.23 us (2%)
    pallas_call x1, Pallas kernels, total_sum(): pl.pallas_call(functools.partial(total_kernel, dp, neg), out_shape=[jax.S...  68.9 us
    pallas_call x2, Pallas kernels, gather(): pl.pallas_call(functools.partial(gather_kernel, sizes, plan), out_shape=[...  23.5 us
    pallas_call x1, Pallas kernels, scatter(): pl.pallas_call(functools.partial(scatter_kernel, sizes, plan), out_shape=...  16 us
    pallas_call x1, Pallas kernels, body(): pl.pallas_call(functools.partial(backward_kernel, per, own), out_shape=[j...  7.92 us
    pallas_call x1, Pallas kernels, body(): pl.pallas_call(functools.partial(forward_kernel, per), out_shape=[jax.Sha...  5.16 us
    concatenate x1, local copies, waits for them, and re-layouts, body(): jnp.concatenate([proj_part.astype(jnp.bfloat16), colbert_part.astype(jnp....  4.31 us
    convert_element_type x1, other arithmetic, body(): summed[:, :width].astype(jnp.float32)  4.07 us

commit v1 on v0

v1 whole, which is shorter than its diff:
```python
import functools

import jax
import jax.numpy as jnp
from jax import lax
from jax.experimental import pallas as pl
from jax.experimental.pallas import tpu as pltpu
from jax.sharding import PartitionSpec as P

MESH = pl.DeviceIdType.MESH
VMEM = pl.BlockSpec(memory_space=pltpu.VMEM)
SMEM = pl.BlockSpec(memory_space=pltpu.SMEM)
ANY = pl.BlockSpec(memory_space=pl.ANY)
LOW = -1e30
F32 = jnp.float32
BF16 = jnp.bfloat16
NT = (((1,), (1,)), ((), ()))
LAG = 3


def exact(a, b, dims=(((1,), (0,)), ((), ()))):
    return lax.dot_general(a, b, dims, precision=lax.Precision.HIGHEST, preferred_element_type=F32)


def each(size, act):
    def turn(k, carry):
        act(k)
        return carry

    lax.fori_loop(1, size, turn, 0)


def loop(low, high, act):
    def turn(k, carry):
        act(k)
        return carry

    lax.fori_loop(low, high, turn, 0)


def remote(src, dst, send, recv, device):
    return pltpu.make_async_remote_copy(
        src_ref=src, dst_ref=dst, send_sem=send, recv_sem=recv, device_id=device, device_id_type=MESH
    )


class Grid:
    def __init__(self, dp, neg):
        groups = neg // 2
        self.dp, self.neg = dp, neg
        self.a = 2 if groups % 2 == 0 else 1
        self.b = groups // self.a
        self.n1, self.n2, self.nz = self.b, self.a, dp
        self.turned = self.a == self.b
        self.n = dp * neg
        self.half = self.n // 2
        self.plane = self.n2 * self.nz

    def locate(self):
        self.r, self.col = lax.axis_index("dp"), lax.axis_index("neg")
        self.core = lax.rem(self.col, 2)
        g = self.col // 2
        self.y, self.x = g // self.b, lax.rem(g, self.b)
        self.me = self.r * self.neg + self.col

    def flip(self, core):
        return core if self.turned else 0 * core

    def own(self, core):
        f = self.flip(core)
        return (self.x * (1 - f) + self.y * f, self.y * (1 - f) + self.x * f)

    def column(self, j1, j2, core):
        f = self.flip(core)
        x, y = j1 * (1 - f) + j2 * f, j2 * (1 - f) + j1 * f
        return (y * self.b + x) * 2 + core

    def nearby(self, k):
        there, bit = self.r, 1
        while bit < self.nz:
            there = there + lax.rem(k // bit, 2) * bit * (1 - 2 * lax.rem(self.r // bit, 2))
            bit *= 2
        return there

    def arrival(self, i, core):
        i1, i2 = self.own(core)
        m2, m1, k = i // (self.n1 * self.nz), lax.rem(i // self.nz, self.n1), lax.rem(i, self.nz)
        return (self.nearby(k), lax.rem(i1 + m1, self.n1), lax.rem(i2 + m2, self.n2))

    def slot(self, rr, j1, j2, core):
        return rr * self.neg + self.column(j1, j2, core)


def main_kernel(dp, neg, own, per, query, positive, passage, lengths, resid, context, out_proj, gain, colbert,
                loss, query_grad, resid_grad, context_grad, sum_main, sum_col,
                q_all, msg, e_all, u_all, sums, inner, scale, bias, flipped, emb_acc,
                res_v, ctx_v, wo_v, cp_v, ctx_t, scaled_t, normed, inv_std, hg, cg,
                q_own, q_snd, q_pl, q_b1, q_l1, q_b2, q_l2, q_b3, q_l3,
                c_own, c_snd, c_pl, c_b1, c_l1, c_b2, c_l2, c_b3, c_l3,
                m_own, m_snd, m_pl, m_b1, m_l1, m_b2, m_l2, m_b3, m_l3,
                ld, zs, a1s, a2s, pps, agr, xs, xr, rs_s, rs_r, ag_s, ag_r, st):
    at = Grid(dp, neg)
    at.locate()
    r, core, me = at.r, at.core, at.me
    other = 1 - core
    i1, i2 = at.own(core)
    n, n1, n2, nz, half, plane = at.n, at.n1, at.n2, at.nz, at.half, at.plane
    place = (i1 * n2 + i2) * nz + r
    partner = (r, at.col + 1 - 2 * core)
    tok = own * per
    wide = n * own
    rows, width = resid.shape
    block = rows // 4
    chunks = sum_main.shape[0]
    cw = sum_main.shape[-1]

    def dev1(t):
        return (r, at.column(lax.rem(i1 + t, n1), i2, core))

    def dev2(t):
        return (r, at.column(i1, lax.rem(i2 + t, n2), core))

    def devz(k):
        return (lax.rem(r + k, nz), at.col)

    def any_device(k):
        d = lax.rem(me + k, n)
        return (d // neg, lax.rem(d, neg))

    loads = [
        pltpu.make_async_copy(context, ctx_v, ld.at[0]),
        pltpu.make_async_copy(out_proj, wo_v, ld.at[1]),
        pltpu.make_async_copy(resid, res_v, ld.at[2]),
        pltpu.make_async_copy(colbert, cp_v, ld.at[3]),
        pltpu.make_async_copy(query, q_all.at[me], ld.at[4]),
    ]
    for copy in loads:
        copy.start()
    barrier = pltpu.get_barrier_semaphore()
    each(n, lambda k: pl.semaphore_signal(barrier, inc=1, device_id=any_device(k), device_id_type=MESH))

    length = lengths[0]
    pas = passage[...]
    position = lax.broadcasted_iota(jnp.int32, bias.shape, 0)
    bias[...] = jnp.where(position < length, 0.0, LOW)
    flipped[...] = pas.astype(F32).T.astype(BF16)
    for copy in loads:
        copy.wait()

    def norm_block(i):
        at_row = pl.multiple_of(i * block, block)
        cut = pl.ds(at_row, block)
        ctx = ctx_v[cut, :]
        hidden = res_v[cut, :].astype(F32) + jnp.dot(ctx, wo_v[...], preferred_element_type=F32)
        centred = hidden - jnp.mean(hidden, axis=1, keepdims=True)
        variance = jnp.mean(centred * centred, axis=1, keepdims=True)
        inv = 1.0 / jnp.sqrt(variance + 1e-05)
        norm = centred * inv
        normed[cut, :] = norm
        inv_std[cut, :] = jnp.broadcast_to(inv, (block, inv_std.shape[1]))
        scaled_t[:, cut] = (norm * gain[...]).T.astype(BF16)
        ctx_t[:, cut] = ctx.astype(F32).T.astype(BF16)

    loop(0, 4, norm_block)
    pl.semaphore_wait(barrier, n - 1)

    def z_copy(k):
        return remote(q_all.at[me], q_all.at[me], zs.at[k], agr.at[me], devz(k))

    def a1_copy(s, rr, t):
        return remote(q_all.at[s], q_all.at[s], a1s.at[rr, t], agr.at[s], dev1(t))

    def a2_copy(s, rr, j1, t):
        return remote(q_all.at[s], q_all.at[s], a2s.at[rr * n1 + j1, t], agr.at[s], dev2(t))

    def pp_copy(s, rr, j1, j2):
        return remote(q_all.at[s], q_all.at[s], pps.at[(j1 * n2 + j2) * nz + rr], agr.at[s], partner)

    def landed(s):
        remote(q_all.at[s], q_all.at[s], zs.at[0], agr.at[s], partner).wait_recv()

    def forward(i):
        rr, j1, j2 = at.arrival(i, core)
        s = at.slot(rr, j1, j2, core)

        @pl.when(i < nz)
        def _():
            each(n1, lambda t: a1_copy(s, rr, t).start())

        @pl.when(i < nz * n1)
        def _():
            each(n2, lambda t: a2_copy(s, rr, j1, t).start())

        pp_copy(s, rr, j1, j2).start()

    def attend(s):
        scores = lax.dot_general(passage[...], q_all[s], NT, preferred_element_type=F32) + bias[...]
        highest = jnp.max(scores, axis=0, keepdims=True)
        spread = jnp.exp(scores - highest)
        total = jnp.sum(spread, axis=0, keepdims=True)
        low = spread.astype(BF16)
        e_all[s] = low
        sums[pl.ds(s, 1), :] = total
        inner[pl.ds(s, 1), :] = highest + jnp.log(total)
        u_all[s] = jnp.dot(flipped[...], low, preferred_element_type=F32)

    def attend_pair(i):
        attend(at.slot(*at.arrival(i, core), core))
        s = at.slot(*at.arrival(i, other), other)
        landed(s)
        attend(s)

    each(nz, lambda k: z_copy(k).start())
    forward(0)

    def relay(i):
        landed(at.slot(*at.arrival(i, core), core))
        forward(i)

        @pl.when(i >= LAG)
        def _():
            attend_pair(i - LAG)

    loop(1, half, relay)
    loop(half - LAG, half, attend_pair)

    token = lax.broadcasted_iota(jnp.int32, (tok, wide), 0)
    lane = lax.broadcasted_iota(jnp.int32, (tok, wide), 1)
    spots = jnp.where(token // per == lax.rem(lane, own), 1.0, 0.0)
    slot_of = lax.broadcasted_iota(jnp.int32, (n, wide), 0)
    lane_of = lax.broadcasted_iota(jnp.int32, (n, wide), 1)
    mine = slot_of == lane_of // own
    grouped = exact(inner[...], spots)
    similar = jnp.sum(jnp.where(mine, grouped, 0.0), axis=0, keepdims=True)
    shift = jnp.log(jnp.full((1, wide), length, jnp.int32).astype(F32)) * per
    row_lane = lax.broadcasted_iota(jnp.int32, (1, wide), 1)
    chosen = jnp.zeros((1, wide), jnp.int32)
    for i in range(own):
        chosen = chosen + jnp.where(row_lane == me * own + i, positive[i], 0)
    msg[me, :, :wide] = similar - shift
    msg[me, :, wide:] = chosen.astype(F32)

    def msg_copy(k, slot):
        return remote(msg.at[slot], msg.at[slot], xs.at[k], xr.at[k], any_device(k))

    each(n, lambda k: msg_copy(k, me).start())
    each(n, lambda k: msg_copy(k, lax.rem(me - k + n, n)).wait_recv())

    everyone = msg[:, :, :wide]
    picked = jnp.sum(msg[:, :, wide:], axis=0)
    highest = jnp.max(everyone, axis=0)
    log_total = highest + jnp.log(jnp.sum(jnp.exp(everyone - highest[None]), axis=0))
    which = lax.broadcasted_iota(jnp.int32, everyone.shape, 0).astype(F32)
    score = jnp.sum(jnp.where(which == picked[None], everyone, 0.0), axis=0)
    average = jnp.sum(log_total - score, axis=1, keepdims=True) / wide
    loss[...] = jnp.broadcast_to(average, loss.shape)
    hit = jnp.where(picked == me.astype(F32), 1.0, 0.0)
    coefficient = jnp.exp(similar - shift - log_total) - hit
    laid = jnp.where(mine, jnp.broadcast_to(coefficient, mine.shape), 0.0)
    scale[...] = exact(laid, spots, NT) / sums[...]

    jobs = [(q_own, q_snd, q_pl, q_b1, q_l1, q_b2, q_l2, q_b3, q_l3, None)]
    jobs += [(c_own, c_snd, c_pl, c_b1, c_l1, c_b2, c_l2, c_b3, c_l3, sum_col)]
    for k in range(chunks):
        jobs.append((m_own.at[k], m_snd.at[k], m_pl.at[k], m_b1.at[k], m_l1.at[k], m_b2.at[k], m_l2.at[k],
                     m_b3.at[k], m_l3.at[k], sum_main.at[k]))

    def pair_copy(j):
        return remote(jobs[j][1], jobs[j][2], rs_s.at[j, 0, 0], rs_r.at[j, 0, 0], partner)

    def rs1_copy(j, t):
        there = pl.ds(lax.rem(i1 + t, n1) * plane, plane)
        return remote(jobs[j][3].at[there], jobs[j][4].at[t], rs_s.at[j, 1, t], rs_r.at[j, 1, t], dev1(t))

    def rs2_copy(j, t):
        there = pl.ds(lax.rem(i2 + t, n2) * nz, nz)
        return remote(jobs[j][5].at[there], jobs[j][6].at[t], rs_s.at[j, 2, t], rs_r.at[j, 2, t], dev2(t))

    def rs3_copy(j, k):
        return remote(jobs[j][7].at[lax.rem(r + k, nz)], jobs[j][8].at[k], rs_s.at[j, 3, k], rs_r.at[j, 3, k], devz(k))

    def ag3_copy(j, k, here):
        piece = jobs[j][9].at[core, here]
        return remote(piece, piece, ag_s.at[j, 0, k], ag_r.at[j, 0, k], devz(k))

    def ag2_copy(j, t, j2):
        piece = jobs[j][9].at[core, pl.ds((i1 * n2 + j2) * nz, nz)]
        return remote(piece, piece, ag_s.at[j, 1, t], ag_r.at[j, 1, t], dev2(t))

    def ag1_copy(j, t, j1):
        piece = jobs[j][9].at[core, pl.ds(j1 * plane, plane)]
        return remote(piece, piece, ag_s.at[j, 2, t], ag_r.at[j, 2, t], dev1(t))

    def ag0_copy(j, c):
        piece = jobs[j][9].at[c]
        return remote(piece, piece, ag_s.at[j, 3, 0], ag_r.at[j, 3, 0], partner)

    def step1(j):
        pair_copy(j).wait_recv()
        job = jobs[j]
        job[3][...] = (job[0][...].astype(F32) + job[2][...].astype(F32)).astype(BF16)
        for t in range(1, n1):
            rs1_copy(j, t).start()

    def step2(j):
        job = jobs[j]
        total = job[3][pl.ds(i1 * plane, plane)].astype(F32)
        for t in range(1, n1):
            rs1_copy(j, t).wait_recv()
            total = total + job[4][t].astype(F32)
        job[5][...] = total.astype(BF16)
        for t in range(1, n2):
            rs2_copy(j, t).start()

    def step3(j):
        job = jobs[j]
        total = job[5][pl.ds(i2 * nz, nz)].astype(F32)
        for t in range(1, n2):
            rs2_copy(j, t).wait_recv()
            total = total + job[6][t].astype(F32)
        job[7][...] = total.astype(BF16)
        for k in range(1, nz):
            rs3_copy(j, k).start()

    def step4(j):
        job = jobs[j]
        total = job[7][r].astype(F32)
        for k in range(1, nz):
            rs3_copy(j, k).wait_recv()
            total = total + job[8][k].astype(F32)
        if job[9] is None:
            query_grad[...] = total.T
        else:
            job[9][core, place] = total.astype(BF16)
            for k in range(1, nz):
                ag3_copy(j, k, place).start()

    def step5(j):
        if jobs[j][9] is None:
            return
        for k in range(1, nz):
            ag3_copy(j, k, (i1 * n2 + i2) * nz + lax.rem(r - k + nz, nz)).wait_recv()
        for t in range(1, n2):
            ag2_copy(j, t, i2).start()

    def step6(j):
        if jobs[j][9] is None:
            return
        for t in range(1, n2):
            ag2_copy(j, t, lax.rem(i2 - t + n2, n2)).wait_recv()
        for t in range(1, n1):
            ag1_copy(j, t, i1).start()

    def step7(j):
        if jobs[j][9] is None:
            return
        for t in range(1, n1):
            ag1_copy(j, t, lax.rem(i1 - t + n1, n1)).wait_recv()
        ag0_copy(j, core).start()

    def step8(j):
        if jobs[j][9] is None:
            return
        ag0_copy(j, other).wait_recv()

    def query_term(p, parity, into):
        j1, j2, rr = p // plane, lax.rem(p // nz, n2), lax.rem(p, nz)
        s = at.slot(rr, j1, j2, parity)
        into[p] = (u_all[s] * scale[pl.ds(s, 1), :]).astype(BF16)

    loop(0, half, lambda p: query_term(p, other, q_snd))
    pair_copy(0).start()

    emb_acc[...] = jnp.zeros_like(emb_acc)

    def emb_term(u):
        parts = []
        for v in range(4):
            s = u * 4 + v
            parts.append((e_all[s].astype(F32) * scale[pl.ds(s, 1), :]).astype(BF16))
        weight = jnp.concatenate(parts, axis=1)
        tokens = q_all[pl.ds(u * 4, 4)].reshape(4 * tok, q_all.shape[2])
        emb_acc[...] += jnp.dot(weight, tokens, preferred_element_type=F32)

    loop(0, n // 4, emb_term)
    emb = emb_acc[...].astype(BF16)
    loop(0, half, lambda p: query_term(p, core, q_own))

    def halves(j, own_half, snd_half):
        jobs[j][1][...] = snd_half.reshape(jobs[j][1].shape).astype(BF16)
        pair_copy(j).start()
        jobs[j][0][...] = own_half.reshape(jobs[j][0].shape).astype(BF16)

    mid = width // 2
    other_rows = pl.ds(pl.multiple_of(other * mid, mid), mid)
    own_rows = pl.ds(pl.multiple_of(core * mid, mid), mid)
    halves(1, jnp.dot(scaled_t[own_rows, :], emb, preferred_element_type=F32),
           jnp.dot(scaled_t[other_rows, :], emb, preferred_element_type=F32))
    step1(0)

    emb_acc[...] = emb.astype(F32)

    def grad_block(i):
        cut = pl.ds(pl.multiple_of(i * block, block), block)
        scaled_grad = lax.dot_general(emb_acc[cut, :].astype(BF16), cp_v[...], NT, preferred_element_type=F32)
        gained = scaled_grad * gain[...]
        norm = normed[cut, :]
        hidden_grad = inv_std[cut, 0:1] * (
            gained
            - jnp.mean(gained, axis=1, keepdims=True)
            - norm * jnp.mean(gained * norm, axis=1, keepdims=True)
        )
        hg[cut, :] = hidden_grad.astype(BF16)

    loop(0, 4, grad_block)
    stores = [pltpu.make_async_copy(hg, resid_grad, st.at[0]), pltpu.make_async_copy(cg, context_grad, st.at[1])]
    stores[0].start()

    steps = [step1, step2, step3, step4, step5, step6, step7, step8]
    done = {0: 1, 1: 0}

    def advance():
        for j in sorted(done):
            if done[j] < len(steps):
                steps[done[j]](j)
                done[j] += 1

    def context_block(i):
        cut = pl.ds(i * block, block)
        cg[cut, :] = lax.dot_general(hg[cut, :], wo_v[...], NT, preferred_element_type=F32).astype(BF16)

    for k in range(chunks):
        columns = slice(k * cw, (k + 1) * cw)
        halves(2 + k, jnp.dot(ctx_t[own_rows, :], hg[:, columns], preferred_element_type=F32),
               jnp.dot(ctx_t[other_rows, :], hg[:, columns], preferred_element_type=F32))
        advance()
        done[2 + k] = 0
    for i in range(4):
        context_block(i)
        advance()
    stores[1].start()
    while any(done[j] < len(steps) for j in done):
        advance()
    for copy in stores:
        copy.wait()

    each(nz, lambda k: z_copy(k).wait_send())

    def drain(i):
        rr, j1, j2 = at.arrival(i, core)
        s = at.slot(rr, j1, j2, core)

        @pl.when(i < nz)
        def _():
            each(n1, lambda t: a1_copy(s, rr, t).wait_send())

        @pl.when(i < nz * n1)
        def _():
            each(n2, lambda t: a2_copy(s, rr, j1, t).wait_send())

        pp_copy(s, rr, j1, j2).wait_send()

    loop(0, half, drain)
    each(n, lambda k: msg_copy(k, me).wait_send())
    for j in range(len(jobs)):
        pair_copy(j).wait_send()
        for t in range(1, n1):
            rs1_copy(j, t).wait_send()
        for t in range(1, n2):
            rs2_copy(j, t).wait_send()
        for k in range(1, nz):
            rs3_copy(j, k).wait_send()
        if jobs[j][9] is not None:
            for k in range(1, nz):
                ag3_copy(j, k, place).wait_send()
            for t in range(1, n2):
                ag2_copy(j, t, i2).wait_send()
            for t in range(1, n1):
                ag1_copy(j, t, i1).wait_send()
            ag0_copy(j, core).wait_send()


def finish_kernel(main, col, gain, colbert, proj_grad, colbert_grad, gain_grad):
    chunks, rows, cw = main.shape
    for k in range(chunks):
        proj_grad[:, k * cw : (k + 1) * cw] = main[k].astype(F32)
    wide = col[...].astype(F32)
    colbert_grad[...] = wide
    ones = jnp.ones((8, wide.shape[1]), F32)
    summed = exact(ones, wide * colbert[...].astype(F32), NT)
    gain_grad[...] = summed[0:1, :] / gain[...]


def job_buffers(at, piece, cols, lead=()):
    shapes = [
        (at.half, piece, cols),
        (at.half, piece, cols),
        (at.half, piece, cols),
        (at.half, piece, cols),
        (at.n1, at.plane, piece, cols),
        (at.plane, piece, cols),
        (at.n2, at.nz, piece, cols),
        (at.nz, piece, cols),
        (at.nz, piece, cols),
    ]
    return [pltpu.VMEM(lead + shape, BF16) for shape in shapes]


def body(sizes, query_emb, positive, passage_emb, lengths, residual, context, out_proj, norm_gain, colbert_proj):
    dp, neg = sizes["dp"], sizes["neg"]
    at = Grid(dp, neg)
    own, per, dim = query_emb.shape
    plen = passage_emb.shape[1]
    rows, width = residual.shape
    tok = own * per
    n = at.n
    chunks = 4
    cw = width // chunks
    piece = width // (2 * at.half)
    dma = pltpu.SemaphoreType.DMA
    vm = pltpu.VMEM
    most = max(at.n1, at.n2, at.nz)
    scratch = [
        vm((n, tok, dim), BF16),
        vm((n, 1, 2 * n * own), F32),
        vm((n, plen, tok), BF16),
        vm((n, dim, tok), F32),
        vm((n, tok), F32),
        vm((n, tok), F32),
        vm((n, tok), F32),
        vm((plen, tok), F32),
        vm((dim, plen), BF16),
        vm((plen, dim), F32),
        vm((rows, width), BF16),
        vm((rows, width), BF16),
        vm((width, width), BF16),
        vm((width, dim), BF16),
        vm((width, rows), BF16),
        vm((width, rows), BF16),
        vm((rows, width), F32),
        vm((rows, 128), F32),
        vm((rows, width), BF16),
        vm((rows, width), BF16),
    ]
    scratch += job_buffers(at, dim, tok)
    scratch += job_buffers(at, piece, dim)
    scratch += job_buffers(at, piece, cw, (chunks,))
    scratch += [
        dma((5,)),
        dma((at.nz,)),
        dma((at.nz, at.n1)),
        dma((at.nz * at.n1, at.n2)),
        dma((at.half,)),
        dma((n,)),
        dma((n,)),
        dma((n,)),
        dma((chunks + 2, 4, most)),
        dma((chunks + 2, 4, most)),
        dma((chunks + 2, 4, most)),
        dma((chunks + 2, 4, most)),
        dma((2,)),
    ]
    loss, query_grad, resid_grad, context_grad, sum_main, sum_col = pl.pallas_call(
        functools.partial(main_kernel, dp, neg, own, per),
        out_shape=[
            jax.ShapeDtypeStruct((1, 128), F32),
            jax.ShapeDtypeStruct((tok, dim), F32),
            jax.ShapeDtypeStruct((rows, width), BF16),
            jax.ShapeDtypeStruct((rows, width), BF16),
            jax.ShapeDtypeStruct((chunks, 2, at.half, piece, cw), BF16),
            jax.ShapeDtypeStruct((2, at.half, piece, dim), BF16),
        ],
        in_specs=[VMEM, SMEM, VMEM, SMEM, ANY, ANY, ANY, VMEM, ANY],
        out_specs=[VMEM, VMEM, ANY, ANY, VMEM, VMEM],
        scratch_shapes=scratch,
        compiler_params=pltpu.CompilerParams(
            collective_id=1, has_side_effects=True, vmem_limit_bytes=67043328
        ),
        name="maxsim_main",
    )(
        query_emb.reshape(tok, dim),
        positive,
        passage_emb.reshape(plen, dim),
        lengths,
        residual,
        context,
        out_proj,
        norm_gain[None, :],
        colbert_proj,
    )
    proj_grad, colbert_grad, gain_grad = pl.pallas_call(
        finish_kernel,
        out_shape=[
            jax.ShapeDtypeStruct((width, width), F32),
            jax.ShapeDtypeStruct((width, dim), F32),
            jax.ShapeDtypeStruct((1, width), F32),
        ],
        in_specs=[VMEM] * 4,
        out_specs=[VMEM] * 3,
        name="maxsim_finish",
    )(
        sum_main.reshape(chunks, width, cw),
        sum_col.reshape(width, dim),
        norm_gain[None, :],
        colbert_proj,
    )
    return (
        loss[0, 0],
        query_grad.reshape(own, per, dim),
        resid_grad,
        context_grad,
        proj_grad,
        colbert_grad,
        gain_grad.reshape(width),
    )


def solution(mesh):
    sizes = {axis: mesh.shape[axis] for axis in ("dp", "neg")}
    split = ("dp", "neg")
    in_specs = (
        P(split, None, None),
        P(split),
        P(split, None, None),
        P(split),
        P(split, None),
        P(split, None),
        P(),
        P(),
        P(),
    )
    out_specs = (
        P(),
        P(split, None, None),
        P(split, None),
        P(split, None),
        P(),
        P(),
        P(),
    )
    return jax.shard_map(
        functools.partial(body, sizes), mesh=mesh, in_specs=in_specs, out_specs=out_specs, check_vma=False
    )
```

time: 151 us -> 104 us (0.69)
  the two profiles are of different devices: /device:TPU:29 before, /device:TPU:0 now
where the time goes in v1:
time: 104 us; the launch traced here: 103 us
  Pallas kernels  97.8 us (94%)
  local copies, waits for them, and re-layouts  2.59 us (2%)
  between operations  2.5 us (2%)
    pallas_call x1, Pallas kernels, body(): pl.pallas_call(functools.partial(main_kernel, dp, neg, own, per), out_sha...  93.3 us
    pallas_call x1, Pallas kernels, body(): pl.pallas_call(finish_kernel, out_shape=[jax.ShapeDtypeStruct((width, wid...  4.53 us
    unnamed x11, local copies, waits for them, and re-layouts  2.59 us

profile of v1, /device:TPU:0, one launch (start us, length us, event | category | flops | bytes accessed | tf_op | source)
XLA Modules:
  0.0 102.9 jit_solution(17023151254597354385)
XLA Ops:
  1.3 93.3 %maxsim_main.1 = (f32[1,128]{1,0:T(1,128)}, f32[128,128]{1,0:T(8,128)}, bf16[512,1024]{1,0:T(8,128)(2,1)}, bf16[512,1024]{1,0:T(8,128)(2,1)}, bf16[4,2,16,32,256...) custom-call(bf16[128,128]{1,0:T(8,128)(2,1)} %bitcast.13, s32[4]{0:T(128)} %positive.1, bf16[512,128]{1,0:T(8,128)(2,1)} %bitcast.11, ...), custom_call_target="tpu_custom_call" | custom-call | tf_op jit(solution)/shard_map/maxsim_main/pallas_call | solution.py:563
  94.6 0.0 copy-start.3
  94.6 0.0 copy-start.2
  94.6 0.0 copy-start.1
  94.6 0.0 copy-start
  94.6 4.5 %maxsim_finish.1 = (f32[1024,1024]{1,0:T(8,128)}, f32[1024,128]{1,0:T(8,128)}, f32[1,1024]{1,0:T(1,128)}) custom-call(bf16[4,1024,256]{2,1,0:T(8,128)(2,1)} %bitcast.9, bf16[1024,128]{1,0:T(8,128)(2,1)} %bitcast.10, f32[1,1024]{1,0:T(1,128)} %bitcast.15, bf16[1024,128]{1,0:T(8,128)(2,1)} %colbert.3), custom_call_target="tpu_custom_call" | custom-call | tf_op jit(solution)/shard_map/maxsim_finish/pallas_call | solution.py:591
  99.2 0.0 copy-done.3
  99.2 0.0 copy-done.2
  99.2 0.6 copy.22
  99.8 0.0 copy-done.1
  99.8 1.0 copy.23
  100.8 0.0 copy-done
  100.8 1.0 copy.24
Async XLA Ops:
  94.6 4.6 %copy-start.3 = (f32[1,128]{1,0:T(1,128)S(1)}, f32[1,128]{1,0:T(1,128)}, u32[]{:S(2)}) copy-start(f32[1,128]{1,0:T(1,128)} %get-tuple-element.16) | copy-start | bytes 1540
  94.6 4.6 %copy-start.2 = (f32[128,128]{1,0:T(8,128)S(1)}, f32[128,128]{1,0:T(8,128)}, u32[]{:S(2)}) copy-start(f32[128,128]{1,0:T(8,128)} %get-tuple-element.17) | copy-start | bytes 196612
  94.6 5.2 %copy-start.1 = (bf16[512,1024]{1,0:T(8,128)(2,1)S(1)}, bf16[512,1024]{1,0:T(8,128)(2,1)}, u32[]{:S(2)}) copy-start(bf16[512,1024]{1,0:T(8,128)(2,1)} %get-tuple-element.34) | copy-start | bytes 3145732
  94.6 6.2 %copy-start = (bf16[512,1024]{1,0:T(8,128)(2,1)S(1)}, bf16[512,1024]{1,0:T(8,128)(2,1)}, u32[]{:S(2)}) copy-start(bf16[512,1024]{1,0:T(8,128)(2,1)} %get-tuple-element.35) | copy-start | bytes 3145732

commit v2 on v1

v2 whole, which is shorter than its diff:
```python
import functools
import math

import jax
import jax.numpy as jnp
from jax import lax
from jax.experimental import pallas as pl
from jax.experimental.pallas import tpu as pltpu
from jax.sharding import PartitionSpec as P

MESH = pl.DeviceIdType.MESH
VMEM = pl.BlockSpec(memory_space=pltpu.VMEM)
SMEM = pl.BlockSpec(memory_space=pltpu.SMEM)
ANY = pl.BlockSpec(memory_space=pl.ANY)
HBM = pl.BlockSpec(memory_space=pltpu.HBM)
LOW = -1e30
F32 = jnp.float32
BF16 = jnp.bfloat16
NT = (((1,), (1,)), ((), ()))
LAG = 1


def exact(a, b, dims=(((1,), (0,)), ((), ()))):
    return lax.dot_general(a, b, dims, precision=lax.Precision.HIGHEST, preferred_element_type=F32)


def each(size, act):
    def turn(k, carry):
        act(k)
        return carry

    lax.fori_loop(1, size, turn, 0)


def loop(low, high, act):
    def turn(k, carry):
        act(k)
        return carry

    lax.fori_loop(low, high, turn, 0)


def remote(src, dst, send, recv, device):
    return pltpu.make_async_remote_copy(
        src_ref=src, dst_ref=dst, send_sem=send, recv_sem=recv, device_id=device, device_id_type=MESH
    )


class Grid:
    def __init__(self, dp, neg):
        groups = neg // 2
        self.dp, self.neg = dp, neg
        self.a = 2 if groups % 2 == 0 else 1
        self.b = groups // self.a
        self.n1, self.n2, self.nz = self.b, self.a, dp
        self.turned = self.a == self.b
        self.n = dp * neg
        self.half = self.n // 2
        self.plane = self.n2 * self.nz

    def locate(self):
        self.r, self.col = lax.axis_index("dp"), lax.axis_index("neg")
        self.core = lax.rem(self.col, 2)
        g = self.col // 2
        self.y, self.x = g // self.b, lax.rem(g, self.b)
        self.me = self.r * self.neg + self.col

    def flip(self, core):
        return core if self.turned else 0 * core

    def own(self, core):
        f = self.flip(core)
        return (self.x * (1 - f) + self.y * f, self.y * (1 - f) + self.x * f)

    def column(self, j1, j2, core):
        f = self.flip(core)
        x, y = j1 * (1 - f) + j2 * f, j2 * (1 - f) + j1 * f
        return (y * self.b + x) * 2 + core

    def nearby(self, k):
        there, bit = self.r, 1
        while bit < self.nz:
            there = there + lax.rem(k // bit, 2) * bit * (1 - 2 * lax.rem(self.r // bit, 2))
            bit *= 2
        return there

    def arrival(self, i, core):
        i1, i2 = self.own(core)
        m2, m1, k = i // (self.n1 * self.nz), lax.rem(i // self.nz, self.n1), lax.rem(i, self.nz)
        return (self.nearby(k), lax.rem(i1 + m1, self.n1), lax.rem(i2 + m2, self.n2))

    def slot(self, rr, j1, j2, core):
        return rr * self.neg + self.column(j1, j2, core)


def main_kernel(dp, neg, own, per, query, positive_in, passage, lengths, resid, context, out_proj, gain_in, colbert,
                loss, query_grad, resid_grad, context_grad, sum_main, sum_col,
                q_all, msg, e_all, u_all, sums, inner, scale, bias, pas_v, flipped, emb_acc,
                positive, gain, wo_v, cp_v, ctx_t, scaled_t, normed, inv_std, *rest):
    at = Grid(dp, neg)
    at.locate()
    r, core, me = at.r, at.core, at.me
    other = 1 - core
    i1, i2 = at.own(core)
    n, n1, n2, nz, half, plane = at.n, at.n1, at.n2, at.nz, at.half, at.plane
    place = (i1 * n2 + i2) * nz + r
    partner = (r, at.col + 1 - 2 * core)
    tok = own * per
    wide = n * own
    rows, width = resid.shape
    block = rows // 4
    chunks = sum_main.shape[0]
    cw = sum_main.shape[-1]
    count = len(JOB)
    sems = rest[3 * count :]
    ld, zs, a1s, a2s, pps, agr, xs, xr, rs_s, rs_r, ag_s, ag_r = sems

    def dev1(t):
        return (r, at.column(lax.rem(i1 + t, n1), i2, core))

    def dev2(t):
        return (r, at.column(i1, lax.rem(i2 + t, n2), core))

    def devz(k):
        return (lax.rem(r + k, nz), at.col)

    def any_device(k):
        d = lax.rem(me + k, n)
        return (d // neg, lax.rem(d, neg))

    barrier = pltpu.get_barrier_semaphore()

    def greet(device):
        pl.semaphore_signal(barrier, inc=1, device_id=device, device_id_type=MESH)

    each(nz, lambda k: greet(devz(k)))
    each(n1, lambda t: greet(dev1(t)))
    each(n2, lambda t: greet(dev2(t)))
    greet(partner)
    loads = [
        pltpu.make_async_copy(query, q_all.at[me], ld.at[0]),
        pltpu.make_async_copy(passage, pas_v, ld.at[1]),
        pltpu.make_async_copy(context, context_grad, ld.at[2]),
        pltpu.make_async_copy(out_proj, wo_v, ld.at[3]),
        pltpu.make_async_copy(resid, resid_grad, ld.at[4]),
        pltpu.make_async_copy(colbert, cp_v, ld.at[5]),
        pltpu.make_async_copy(gain_in, gain, ld.at[7]),
        pltpu.make_async_copy(positive_in, positive, ld.at[8]),
    ]
    for copy in loads:
        copy.start()
    loads[0].wait()
    pl.semaphore_wait(barrier, nz + n1 + n2 - 2)

    def z_copy(k):
        return remote(q_all.at[me], q_all.at[me], zs.at[k], agr.at[me], devz(k))

    def a1_copy(s, rr, t):
        return remote(q_all.at[s], q_all.at[s], a1s.at[rr, t], agr.at[s], dev1(t))

    def a2_copy(s, rr, j1, t):
        return remote(q_all.at[s], q_all.at[s], a2s.at[rr * n1 + j1, t], agr.at[s], dev2(t))

    def pp_copy(s, rr, j1, j2):
        return remote(q_all.at[s], q_all.at[s], pps.at[(j1 * n2 + j2) * nz + rr], agr.at[s], partner)

    def landed(s):
        remote(q_all.at[s], q_all.at[s], zs.at[0], agr.at[s], partner).wait_recv()

    def route(i, act):
        rr, j1, j2 = at.arrival(i, core)
        s = at.slot(rr, j1, j2, core)

        @pl.when(i < nz)
        def _():
            each(n1, lambda t: act(a1_copy(s, rr, t)))

        @pl.when(i < nz * n1)
        def _():
            each(n2, lambda t: act(a2_copy(s, rr, j1, t)))

        act(pp_copy(s, rr, j1, j2))

    def attend(slots):
        tokens = jnp.concatenate([q_all[s] for s in slots], axis=0)
        scores = lax.dot_general(pas_v[...], tokens, NT, preferred_element_type=F32) + bias[...]
        highest = jnp.max(scores, axis=0, keepdims=True)
        spread = jnp.exp(scores - highest)
        total = jnp.sum(spread, axis=0, keepdims=True)
        low = spread.astype(BF16)
        level = highest + jnp.log(total)
        below = jnp.dot(flipped[...], low, preferred_element_type=F32)
        for v, s in enumerate(slots):
            cut = slice(v * tok, (v + 1) * tok)
            e_all[s] = low[:, cut]
            sums[pl.ds(s, 1), :] = total[:, cut]
            inner[pl.ds(s, 1), :] = level[:, cut]
            u_all[s] = below[:, cut]

    def attend_group(u):
        mine = [at.slot(*at.arrival(2 * u + v, core), core) for v in range(2)]
        theirs = [at.slot(*at.arrival(2 * u + v, other), other) for v in range(2)]
        for s in theirs:
            landed(s)
        attend(mine)
        attend(theirs)

    each(nz, lambda k: z_copy(k).start())
    route(0, lambda copy: copy.start())
    loads[1].wait()
    length = lengths[0]
    position = lax.broadcasted_iota(jnp.int32, bias.shape, 0)
    bias[...] = jnp.where(position < length, 0.0, LOW)
    flipped[...] = pas_v[...].astype(F32).T.astype(BF16)

    def relay(i):
        landed(at.slot(*at.arrival(i, core), core))
        route(i, lambda copy: copy.start())

    def relay_group(u):
        @pl.when(u > 0)
        def _():
            relay(2 * u)

        relay(2 * u + 1)

        @pl.when(u >= LAG)
        def _():
            attend_group(u - LAG)

    loop(0, half // 2, relay_group)
    loop(half // 2 - LAG, half // 2, attend_group)

    loads[7].wait()
    token = lax.broadcasted_iota(jnp.int32, (tok, wide), 0)
    lane = lax.broadcasted_iota(jnp.int32, (tok, wide), 1)
    spots = jnp.where(token // per == lax.rem(lane, own), 1.0, 0.0)
    slot_of = lax.broadcasted_iota(jnp.int32, (n, wide), 0)
    lane_of = lax.broadcasted_iota(jnp.int32, (n, wide), 1)
    mine = slot_of == lane_of // own
    grouped = exact(inner[...], spots)
    similar = jnp.sum(jnp.where(mine, grouped, 0.0), axis=0, keepdims=True)
    shift = jnp.log(jnp.full((1, wide), length, jnp.int32).astype(F32)) * per
    row_lane = lax.broadcasted_iota(jnp.int32, (1, wide), 1)
    chosen = jnp.zeros((1, wide), jnp.int32)
    for i in range(own):
        chosen = chosen + jnp.where(row_lane == me * own + i, positive[i], 0)
    msg[me, :, :wide] = similar - shift
    msg[me, :, wide:] = chosen.astype(F32)

    def msg_copy(k, slot):
        return remote(msg.at[slot], msg.at[slot], xs.at[k], xr.at[k], any_device(k))

    each(n, lambda k: msg_copy(k, me).start())

    for copy in loads[2:7]:
        copy.wait()

    def norm_block(i):
        cut = pl.ds(pl.multiple_of(i * block, block), block)
        ctx = context_grad[cut, :]
        hidden = resid_grad[cut, :].astype(F32) + jnp.dot(ctx, wo_v[...], preferred_element_type=F32)
        centred = hidden - jnp.mean(hidden, axis=1, keepdims=True)
        variance = jnp.mean(centred * centred, axis=1, keepdims=True)
        inv = 1.0 / jnp.sqrt(variance + 1e-05)
        norm = centred * inv
        normed[cut, :] = norm
        inv_std[cut, :] = jnp.broadcast_to(inv, (block, inv_std.shape[1]))
        scaled_t[:, cut] = (norm * gain[...]).T.astype(BF16)
        ctx_t[:, cut] = ctx.astype(F32).T.astype(BF16)

    loop(0, 4, norm_block)
    each(nz, lambda k: z_copy(k).wait_send())
    loop(0, half, lambda i: route(i, lambda copy: copy.wait_send()))
    each(n, lambda k: msg_copy(k, lax.rem(me - k + n, n)).wait_recv())

    everyone = msg[:, :, :wide]
    picked = jnp.sum(msg[:, :, wide:], axis=0)
    highest = jnp.max(everyone, axis=0)
    log_total = highest + jnp.log(jnp.sum(jnp.exp(everyone - highest[None]), axis=0))
    which = lax.broadcasted_iota(jnp.int32, everyone.shape, 0).astype(F32)
    score = jnp.sum(jnp.where(which == picked[None], everyone, 0.0), axis=0)
    average = jnp.sum(log_total - score, axis=1, keepdims=True) / wide
    loss[...] = jnp.broadcast_to(average, loss.shape)
    hit = jnp.where(picked == me.astype(F32), 1.0, 0.0)
    coefficient = jnp.exp(similar - shift - log_total) - hit
    laid = jnp.where(mine, jnp.broadcast_to(coefficient, mine.shape), 0.0)
    scale[...] = exact(laid, spots, NT) / sums[...]

    jobs = []
    for which_job, out in ((0, None), (1, sum_col)):
        jobs.append(dict(zip(JOB, rest[which_job * count : (which_job + 1) * count]), out=out))
    for k in range(chunks):
        jobs.append(dict(zip(JOB, [ref.at[k] for ref in rest[2 * count : 3 * count]]), out=sum_main.at[k]))

    def pair_copy(j):
        return remote(jobs[j]["snd"], jobs[j]["pl"], rs_s.at[j, 0, 0], rs_r.at[j, 0, 0], partner)

    def rs1_copy(j, t):
        there = pl.ds(lax.rem(i1 + t, n1) * plane, plane)
        return remote(jobs[j]["b1"].at[there], jobs[j]["l1"].at[t], rs_s.at[j, 1, t], rs_r.at[j, 1, t], dev1(t))

    def rs2_copy(j, t):
        there = pl.ds(lax.rem(i2 + t, n2) * nz, nz)
        return remote(jobs[j]["b2"].at[there], jobs[j]["l2"].at[t], rs_s.at[j, 2, t], rs_r.at[j, 2, t], dev2(t))

    def rs3_copy(j, k):
        return remote(jobs[j]["b3"].at[lax.rem(r + k, nz)], jobs[j]["l3"].at[k], rs_s.at[j, 3, k], rs_r.at[j, 3, k], devz(k))

    def ag3_copy(j, k, here):
        piece = jobs[j]["out"].at[core, here]
        return remote(piece, piece, ag_s.at[j, 0, k], ag_r.at[j, 0, k], devz(k))

    def ag2_copy(j, t, j2):
        piece = jobs[j]["out"].at[core, pl.ds((i1 * n2 + j2) * nz, nz)]
        return remote(piece, piece, ag_s.at[j, 1, t], ag_r.at[j, 1, t], dev2(t))

    def ag1_copy(j, t, j1):
        piece = jobs[j]["out"].at[core, pl.ds(j1 * plane, plane)]
        return remote(piece, piece, ag_s.at[j, 2, t], ag_r.at[j, 2, t], dev1(t))

    def ag0_copy(j, c):
        piece = jobs[j]["out"].at[c]
        return remote(piece, piece, ag_s.at[j, 3, 0], ag_r.at[j, 3, 0], partner)

    def step1(j):
        job = jobs[j]
        pair_copy(j).wait_recv()
        if j > 0:
            job["b1"][...] = (job["own"][...] + job["pl"][...].astype(F32)).astype(BF16)
            kept = pl.ds(i1 * plane, plane)
            job["k1"][...] = job["own"][kept] + job["pl"][kept].astype(F32)
        else:

            def send_term(p):
                j1, j2, rr = p // plane, lax.rem(p // nz, n2), lax.rem(p, nz)
                s = at.slot(rr, j1, j2, core)
                total = u_all[s] * scale[pl.ds(s, 1), :] + job["pl"][p].astype(F32)
                job["b1"][p] = total.astype(BF16)

            def keep_term(q):
                p = i1 * plane + q
                j1, j2, rr = p // plane, lax.rem(p // nz, n2), lax.rem(p, nz)
                s = at.slot(rr, j1, j2, core)
                job["k1"][q] = u_all[s] * scale[pl.ds(s, 1), :] + job["pl"][p].astype(F32)

            loop(plane, half, lambda p: send_term(lax.rem(i1 * plane + p, half)))
            loop(0, plane, keep_term)
        for t in range(1, n1):
            rs1_copy(j, t).start()

    def step2(j):
        job = jobs[j]
        total = job["k1"][...]
        for t in range(1, n1):
            rs1_copy(j, t).wait_recv()
            total = total + job["l1"][t].astype(F32)
        job["b2"][...] = total.astype(BF16)
        job["k1"][...] = total
        for t in range(1, n2):
            rs2_copy(j, t).start()

    def step3(j):
        job = jobs[j]
        total = job["k1"][pl.ds(i2 * nz, nz)]
        for t in range(1, n2):
            rs2_copy(j, t).wait_recv()
            total = total + job["l2"][t].astype(F32)
        job["b3"][...] = total.astype(BF16)
        job["k2"][...] = total
        for k in range(1, nz):
            rs3_copy(j, k).start()

    def step4(j):
        job = jobs[j]
        total = job["k2"][r]
        for k in range(1, nz):
            rs3_copy(j, k).wait_recv()
            total = total + job["l3"][k].astype(F32)
        if job["out"] is None:
            query_grad[...] = total.T
        else:
            job["out"][core, place] = total.astype(BF16)
            for k in range(1, nz):
                ag3_copy(j, k, place).start()

    def step5(j):
        for k in range(1, nz):
            ag3_copy(j, k, (i1 * n2 + i2) * nz + lax.rem(r - k + nz, nz)).wait_recv()
        for t in range(1, n2):
            ag2_copy(j, t, i2).start()

    def step6(j):
        for t in range(1, n2):
            ag2_copy(j, t, lax.rem(i2 - t + n2, n2)).wait_recv()
        for t in range(1, n1):
            ag1_copy(j, t, i1).start()

    def step7(j):
        for t in range(1, n1):
            ag1_copy(j, t, lax.rem(i1 - t + n1, n1)).wait_recv()
        ag0_copy(j, core).start()

    def step8(j):
        ag0_copy(j, other).wait_recv()

    def drain_sum(j):
        pair_copy(j).wait_send()
        for t in range(1, n1):
            rs1_copy(j, t).wait_send()
        for t in range(1, n2):
            rs2_copy(j, t).wait_send()
        for k in range(1, nz):
            rs3_copy(j, k).wait_send()

    def drain_out(j):
        for k in range(1, nz):
            ag3_copy(j, k, place).wait_send()
        for t in range(1, n2):
            ag2_copy(j, t, i2).wait_send()
        for t in range(1, n1):
            ag1_copy(j, t, i1).wait_send()
        ag0_copy(j, core).wait_send()

    def query_term(p):
        j1, j2, rr = p // plane, lax.rem(p // nz, n2), lax.rem(p, nz)
        s = at.slot(rr, j1, j2, other)
        jobs[0]["snd"][p] = (u_all[s] * scale[pl.ds(s, 1), :]).astype(BF16)

    loop(0, half, query_term)
    pair_copy(0).start()

    emb_acc[...] = jnp.zeros_like(emb_acc)

    def emb_term(u):
        parts = []
        for v in range(8):
            s = u * 8 + v
            row = jnp.broadcast_to(scale[pl.ds(s, 1), :], (16, tok)).astype(BF16)
            spread = e_all[s]
            parts.append((spread.reshape(-1, 16, tok) * row[None]).reshape(spread.shape))
        weight = jnp.concatenate(parts, axis=1)
        tokens = q_all[pl.ds(u * 8, 8)].reshape(8 * tok, q_all.shape[2])
        emb_acc[...] += jnp.dot(weight, tokens, preferred_element_type=F32)

    loop(0, n // 8, emb_term)
    emb = emb_acc[...].astype(BF16)

    def halves(j, left, right):
        job = jobs[j]
        job["snd"][...] = jnp.dot(left(other), right, preferred_element_type=F32).reshape(job["snd"].shape).astype(BF16)
        pair_copy(j).start()
        job["own"][...] = jnp.dot(left(core), right, preferred_element_type=F32).reshape(job["own"].shape)

    mid = width // 2

    def half_rows(ref):
        return lambda c: ref[pl.ds(pl.multiple_of(c * mid, mid), mid), :]

    halves(1, half_rows(scaled_t), emb)
    emb_acc[...] = emb.astype(F32)
    step1(0)

    def grad_block(i):
        cut = pl.ds(pl.multiple_of(i * block, block), block)
        scaled_grad = lax.dot_general(emb_acc[cut, :].astype(BF16), cp_v[...], NT, preferred_element_type=F32)
        gained = scaled_grad * gain[...]
        norm = normed[cut, :]
        hidden_grad = inv_std[cut, 0:1] * (
            gained
            - jnp.mean(gained, axis=1, keepdims=True)
            - norm * jnp.mean(gained * norm, axis=1, keepdims=True)
        )
        resid_grad[cut, :] = hidden_grad.astype(BF16)

    loop(0, 4, grad_block)

    def context_block(i):
        cut = pl.ds(i * block, block)
        context_grad[cut, :] = lax.dot_general(
            resid_grad[cut, :], wo_v[...], NT, preferred_element_type=F32
        ).astype(BF16)

    step1(1)
    for k in range(chunks):
        halves(2 + k, half_rows(ctx_t), resid_grad[:, k * cw : (k + 1) * cw])
        if k > 0:
            step1(1 + k)
    context_block(0)
    step1(1 + chunks)
    steps = [None, step1, step2, step3, step4, step5, step6, step7, step8]
    order = sorted((j + s, j, s) for j in range(1, chunks + 2) for s in range(2, 9))
    late = chunks + 1
    fillers = 1
    for tick, j, s in order:
        if j == 1 and fillers < 4:
            context_block(fillers)
            fillers += 1
        if j == late and s == 4:
            step2(0)
        if j == late and s == 6:
            step3(0)
        if j == late and s == 7:
            step4(0)
        if j == late and s == 8:
            each(n, lambda k: msg_copy(k, me).wait_send())
            for k in range(chunks + 2):
                drain_sum(k)
            for k in range(1, chunks + 1):
                drain_out(k)
        steps[s](j)
    drain_out(late)


JOB = ("own", "snd", "pl", "b1", "k1", "l1", "b2", "l2", "b3", "k2", "l3")


def finish_kernel(main, col, gain, colbert, loss_in, query_in, resid_in, context_in,
                  proj_grad, colbert_grad, gain_grad, loss, query_grad, resid_grad, context_grad, proj_v, sem):
    copies = [
        pltpu.make_async_copy(resid_in, resid_grad, sem.at[0]),
        pltpu.make_async_copy(context_in, context_grad, sem.at[1]),
        pltpu.make_async_copy(query_in, query_grad, sem.at[2]),
    ]
    for copy in copies:
        copy.start()
    chunks, rows, cw = main.shape
    band = rows // 4
    for b in range(4):
        cut = slice(b * band, (b + 1) * band)
        for k in range(chunks):
            proj_v[cut, k * cw : (k + 1) * cw] = main[k, cut, :].astype(F32)
        copy = pltpu.make_async_copy(proj_v.at[cut], proj_grad.at[cut], sem.at[3 + b])
        copy.start()
        copies.append(copy)
    wide = col[...].astype(F32)
    colbert_grad[...] = wide
    ones = jnp.ones((8, wide.shape[1]), F32)
    summed = exact(ones, wide * colbert[...].astype(F32), NT)
    gain_grad[...] = summed[0:1, :] / gain[...]
    loss[...] = loss_in[:, 0:1]
    for copy in copies:
        copy.wait()


def stay(array):
    return pltpu.with_memory_space_constraint(array, pltpu.HBM)


def job_buffers(at, piece, cols, lead=(), own=True):
    shapes = [
        ((at.half if own else 1, piece, cols), F32),
        ((at.half, piece, cols), BF16),
        ((at.half, piece, cols), BF16),
        ((at.half, piece, cols), BF16),
        ((at.plane, piece, cols), F32),
        ((at.n1, at.plane, piece, cols), BF16),
        ((at.plane, piece, cols), BF16),
        ((at.n2, at.nz, piece, cols), BF16),
        ((at.nz, piece, cols), BF16),
        ((at.nz, piece, cols), F32),
        ((at.nz, piece, cols), BF16),
    ]
    return [pltpu.VMEM(lead + shape, kind) for shape, kind in shapes]


def body(sizes, query_emb, positive, passage_emb, lengths, residual, context, out_proj, norm_gain, colbert_proj):
    dp, neg = sizes["dp"], sizes["neg"]
    at = Grid(dp, neg)
    own, per, dim = query_emb.shape
    plen = passage_emb.shape[1]
    rows, width = residual.shape
    tok = own * per
    n = at.n
    chunks = 4
    cw = width // chunks
    piece = width // (2 * at.half)
    dma = pltpu.SemaphoreType.DMA
    vm = pltpu.VMEM
    most = max(at.n1, at.n2, at.nz)
    scratch = [
        vm((n, tok, dim), BF16),
        vm((n, 1, 2 * n * own), F32),
        vm((n, plen, tok), BF16),
        vm((n, dim, tok), F32),
        vm((n, tok), F32),
        vm((n, tok), F32),
        vm((n, tok), F32),
        vm((plen, 2 * tok), F32),
        vm((plen, dim), BF16),
        vm((dim, plen), BF16),
        vm((plen, dim), F32),
        pltpu.SMEM((own,), jnp.int32),
        vm((1, width), F32),
        vm((width, width), BF16),
        vm((width, dim), BF16),
        vm((width, rows), BF16),
        vm((width, rows), BF16),
        vm((rows, width), F32),
        vm((rows, 128), F32),
    ]
    scratch += job_buffers(at, dim, tok, own=False)
    scratch += job_buffers(at, piece, dim)
    scratch += job_buffers(at, piece, cw, (chunks,))
    scratch += [
        dma((9,)),
        dma((at.nz,)),
        dma((at.nz, at.n1)),
        dma((at.nz * at.n1, at.n2)),
        dma((at.half,)),
        dma((n,)),
        dma((n,)),
        dma((n,)),
        dma((chunks + 2, 4, most)),
        dma((chunks + 2, 4, most)),
        dma((chunks + 2, 4, most)),
        dma((chunks + 2, 4, most)),
    ]
    held = sum(math.prod(ref.shape) * jnp.dtype(ref.dtype).itemsize for ref in scratch[:-12])
    limit = min(held + held // 8 + 8 * 1024 * 1024, 67043328)
    loss, query_grad, resid_grad, context_grad, sum_main, sum_col = pl.pallas_call(
        functools.partial(main_kernel, dp, neg, own, per),
        out_shape=[
            jax.ShapeDtypeStruct((1, 128), F32),
            jax.ShapeDtypeStruct((tok, dim), F32),
            jax.ShapeDtypeStruct((rows, width), BF16),
            jax.ShapeDtypeStruct((rows, width), BF16),
            jax.ShapeDtypeStruct((chunks, 2, at.half, piece, cw), BF16),
            jax.ShapeDtypeStruct((2, at.half, piece, dim), BF16),
        ],
        in_specs=[HBM, HBM, HBM, SMEM, HBM, HBM, HBM, HBM, HBM],
        out_specs=[VMEM] * 6,
        scratch_shapes=scratch,
        compiler_params=pltpu.CompilerParams(
            collective_id=1, has_side_effects=True, vmem_limit_bytes=limit
        ),
        name="maxsim_main",
    )(
        stay(query_emb.reshape(tok, dim)),
        stay(positive),
        stay(passage_emb.reshape(plen, dim)),
        lengths,
        stay(residual),
        stay(context),
        stay(out_proj),
        stay(norm_gain[None, :]),
        stay(colbert_proj),
    )
    proj_grad, colbert_grad, gain_grad, loss, query_grad, resid_grad, context_grad = pl.pallas_call(
        finish_kernel,
        out_shape=[
            jax.ShapeDtypeStruct((width, width), F32),
            jax.ShapeDtypeStruct((width, dim), F32),
            jax.ShapeDtypeStruct((1, width), F32),
            jax.ShapeDtypeStruct((1, 1), F32),
            jax.ShapeDtypeStruct((tok, dim), F32),
            jax.ShapeDtypeStruct((rows, width), BF16),
            jax.ShapeDtypeStruct((rows, width), BF16),
        ],
        in_specs=[VMEM] * 8,
        out_specs=[ANY, VMEM, VMEM, VMEM, ANY, ANY, ANY],
        scratch_shapes=[vm((width, width), F32), dma((7,))],
        compiler_params=pltpu.CompilerParams(vmem_limit_bytes=20000000),
        name="maxsim_finish",
    )(
        sum_main.reshape(chunks, width, cw),
        sum_col.reshape(width, dim),
        norm_gain[None, :],
        colbert_proj,
        loss,
        query_grad,
        resid_grad,
        context_grad,
    )
    return (
        loss.reshape(()),
        query_grad.reshape(own, per, dim),
        resid_grad,
        context_grad,
        proj_grad,
        colbert_grad,
        gain_grad.reshape(width),
    )


def solution(mesh):
    sizes = {axis: mesh.shape[axis] for axis in ("dp", "neg")}
    split = ("dp", "neg")
    in_specs = (
        P(split, None, None),
        P(split),
        P(split, None, None),
        P(split),
        P(split, None),
        P(split, None),
        P(),
        P(),
        P(),
    )
    out_specs = (
        P(),
        P(split, None, None),
        P(split, None),
        P(split, None),
        P(),
        P(),
        P(),
    )
    return jax.shard_map(
        functools.partial(body, sizes), mesh=mesh, in_specs=in_specs, out_specs=out_specs, check_vma=False
    )
```

time: 104 us -> 83.7 us (0.80)
  Pallas kernels: 97.8 us -> 82.2 us
  local copies, waits for them, and re-layouts: 2.59 us -> 0.01 us
  between operations: 2.5 us -> 1.32 us
    pallas_call x1, Pallas kernels: 93.3 us -> 78.5 us  [body(): pl.pallas_call(functools.partial(main_kernel, dp, neg, own, per), out_sha...]
    unnamed x11 -> x4, local copies, waits for them, and re-layouts: 2.59 us -> 0.01 us
where the time goes in v2:
time: 83.7 us; the launch traced here: 83.5 us
  Pallas kernels  82.2 us (98%)
  between operations  1.32 us (2%)
    pallas_call x1, Pallas kernels, body(): pl.pallas_call(functools.partial(main_kernel, dp, neg, own, per), out_sha...  78.5 us
    pallas_call x1, Pallas kernels, body(): pl.pallas_call(finish_kernel, out_shape=[jax.ShapeDtypeStruct((width, wid...  3.75 us

profile of v2, /device:TPU:0, one launch (start us, length us, event | category | flops | bytes accessed | tf_op | source)
XLA Modules:
  0.0 83.5 jit_solution(1310667188046482754)
XLA Ops:
  1.3 0.0 copy-start
  1.3 0.0 copy-start.1
  1.3 78.5 %maxsim_main.1 = (f32[1,128]{1,0:T(1,128)S(1)}, f32[128,128]{1,0:T(8,128)S(1)}, bf16[512,1024]{1,0:T(8,128)(2,1)S(1)}, bf16[512,1024]{1,0:T(8,128)(2,1)S(1)}, bf...) custom-call(bf16[128,128]{1,0:T(8,128)(2,1)} %bitcast.13, s32[4]{0:T(128)} %positive_in.1, ...), custom_call_target="tpu_custom_call" | custom-call | tf_op jit(solution)/shard_map/maxsim_main/pallas_call | solution.py:621
  79.8 0.0 copy-done
  79.8 0.0 copy-done.1
  79.8 3.7 %maxsim_finish.1 = (f32[1024,1024]{1,0:T(8,128)}, f32[1024,128]{1,0:T(8,128)}, f32[1,1024]{1,0:T(1,128)}, f32[1,1]{1,0:T(1,128)}, f32[128,128]{1,0:T(8,128)}, /*...) custom-call(bf16[4,1024,256]{2,1,0:T(8,128)(2,1)S(1)} %bitcast.8, bf16[1024,128]{1,0:T(8,128)(2,1)S(1)} %bitcast.9, ...), custom_call_target="tpu_custom_call" | custom-call | tf_op jit(solution)/shard_map/maxsim_finish/pallas_call | solution.py:649
Async XLA Ops:
  1.3 78.5 %copy-start = (bf16[1024,128]{1,0:T(8,128)(2,1)S(1)}, bf16[1024,128]{1,0:T(8,128)(2,1)}, u32[]{:S(2)}) copy-start(bf16[1024,128]{1,0:T(8,128)(2,1)} %colbert.3) | copy-start | bytes 786436
  1.3 78.5 %copy-start.1 = (f32[1024]{0:T(1024)S(1)}, f32[1024]{0:T(1024)}, u32[]{:S(2)}) copy-start(f32[1024]{0:T(1024)} %param.16) | copy-start | bytes 12292

commit v3 on v2

--- a/solution.py
+++ b/solution.py
@@ -17,7 +17,12 @@
 F32 = jnp.float32
 BF16 = jnp.bfloat16
 NT = (((1,), (1,)), ((), ()))
-LAG = 1
+LAG = 2
+ORDER = (
+    21, -1, 41, -1, 51, -1, -1, -1, 91, -1, 22, -1, 42, 61, -1, 52, 71, -1, 92, 23, 81, 62, 31, 11, 43, 53, 72, 93, 63,
+    24, 82, 44, 32, 1, 73, 54, 94, 83, 33, 12, 25, 45, 74, 55, 2, 13, 46, 64, 84, 95, 34, 56, 14, 75, 26, 3, 65, 96, 85,
+    76, 35, 15, 66, 57, 97, 86, 36, 47, 16, 48, 77, 27, 67, 87, 58, 37, 17, 78, 98, 88, 28, 4, 68, 38, 18,
+)
 
 
 def exact(a, b, dims=(((1,), (0,)), ((), ()))):
@@ -96,7 +101,7 @@
 def main_kernel(dp, neg, own, per, query, positive_in, passage, lengths, resid, context, out_proj, gain_in, colbert,
                 loss, query_grad, resid_grad, context_grad, sum_main, sum_col,
                 q_all, msg, e_all, u_all, sums, inner, scale, bias, pas_v, flipped, emb_acc,
-                positive, gain, wo_v, cp_v, ctx_t, scaled_t, normed, inv_std, *rest):
+                positive, gain, wo_v, cp_v, ctx_t, scaled_t, normed, inv_std, blend, *rest):
     at = Grid(dp, neg)
     at.locate()
     r, core, me = at.r, at.core, at.me
@@ -181,7 +186,16 @@
 
         act(pp_copy(s, rr, j1, j2))
 
-    def attend(slots):
+    def attend(v):
+        u, side = v // 2, lax.rem(v, 2)
+        whose = core * (1 - side) + other * side
+        slots = [at.slot(*at.arrival(2 * u + w, whose), whose) for w in range(2)]
+
+        @pl.when(side == 1)
+        def _():
+            for s in slots:
+                landed(s)
+
         tokens = jnp.concatenate([q_all[s] for s in slots], axis=0)
         scores = lax.dot_general(pas_v[...], tokens, NT, preferred_element_type=F32) + bias[...]
         highest = jnp.max(scores, axis=0, keepdims=True)
@@ -189,21 +203,11 @@
         total = jnp.sum(spread, axis=0, keepdims=True)
         low = spread.astype(BF16)
         level = highest + jnp.log(total)
-        below = jnp.dot(flipped[...], low, preferred_element_type=F32)
-        for v, s in enumerate(slots):
-            cut = slice(v * tok, (v + 1) * tok)
+        for w, s in enumerate(slots):
+            cut = slice(w * tok, (w + 1) * tok)
             e_all[s] = low[:, cut]
             sums[pl.ds(s, 1), :] = total[:, cut]
             inner[pl.ds(s, 1), :] = level[:, cut]
-            u_all[s] = below[:, cut]
-
-    def attend_group(u):
-        mine = [at.slot(*at.arrival(2 * u + v, core), core) for v in range(2)]
-        theirs = [at.slot(*at.arrival(2 * u + v, other), other) for v in range(2)]
-        for s in theirs:
-            landed(s)
-        attend(mine)
-        attend(theirs)
 
     each(nz, lambda k: z_copy(k).start())
     route(0, lambda copy: copy.start())
@@ -217,19 +221,15 @@
         landed(at.slot(*at.arrival(i, core), core))
         route(i, lambda copy: copy.start())
 
-    def relay_group(u):
-        @pl.when(u > 0)
+    def relay_step(i):
+        relay(i)
+
+        @pl.when(i >= LAG)
         def _():
-            relay(2 * u)
-
-        relay(2 * u + 1)
-
-        @pl.when(u >= LAG)
-        def _():
-            attend_group(u - LAG)
-
-    loop(0, half // 2, relay_group)
-    loop(half // 2 - LAG, half // 2, attend_group)
+            attend(i - LAG)
+
+    loop(1, half, relay_step)
+    loop(half - LAG, half, attend)
 
     loads[7].wait()
     token = lax.broadcasted_iota(jnp.int32, (tok, wide), 0)
@@ -266,12 +266,14 @@
         norm = centred * inv
         normed[cut, :] = norm
         inv_std[cut, :] = jnp.broadcast_to(inv, (block, inv_std.shape[1]))
-        scaled_t[:, cut] = (norm * gain[...]).T.astype(BF16)
+        scaled = norm * gain[...]
+        scaled_t[:, cut] = scaled.T.astype(BF16)
+        blend[cut, :] = jnp.dot(scaled.astype(BF16), cp_v[...], preferred_element_type=F32) / width
         ctx_t[:, cut] = ctx.astype(F32).T.astype(BF16)
 
     loop(0, 4, norm_block)
-    each(nz, lambda k: z_copy(k).wait_send())
-    loop(0, half, lambda i: route(i, lambda copy: copy.wait_send()))
+    flat = exact(jnp.broadcast_to(gain[...], (8, width)), cp_v[...].astype(F32))[0:1, :] / width
+
     each(n, lambda k: msg_copy(k, lax.rem(me - k + n, n)).wait_recv())
 
     everyone = msg[:, :, :wide]
@@ -422,94 +424,111 @@
             ag1_copy(j, t, i1).wait_send()
         ag0_copy(j, core).wait_send()
 
-    def query_term(p):
-        j1, j2, rr = p // plane, lax.rem(p // nz, n2), lax.rem(p, nz)
-        s = at.slot(rr, j1, j2, other)
-        jobs[0]["snd"][p] = (u_all[s] * scale[pl.ds(s, 1), :]).astype(BF16)
-
-    loop(0, half, query_term)
-    pair_copy(0).start()
-
     emb_acc[...] = jnp.zeros_like(emb_acc)
 
     def emb_term(u):
         parts = []
-        for v in range(8):
-            s = u * 8 + v
+        for v in range(16):
+            s = u * 16 + v
             row = jnp.broadcast_to(scale[pl.ds(s, 1), :], (16, tok)).astype(BF16)
             spread = e_all[s]
             parts.append((spread.reshape(-1, 16, tok) * row[None]).reshape(spread.shape))
         weight = jnp.concatenate(parts, axis=1)
-        tokens = q_all[pl.ds(u * 8, 8)].reshape(8 * tok, q_all.shape[2])
+        tokens = q_all[pl.ds(u * 16, 16)].reshape(16 * tok, q_all.shape[2])
         emb_acc[...] += jnp.dot(weight, tokens, preferred_element_type=F32)
 
-    loop(0, n // 8, emb_term)
+    loop(0, n // 16, emb_term)
     emb = emb_acc[...].astype(BF16)
-
-    def halves(j, left, right):
-        job = jobs[j]
-        job["snd"][...] = jnp.dot(left(other), right, preferred_element_type=F32).reshape(job["snd"].shape).astype(BF16)
-        pair_copy(j).start()
-        job["own"][...] = jnp.dot(left(core), right, preferred_element_type=F32).reshape(job["own"].shape)
-
-    mid = width // 2
-
-    def half_rows(ref):
-        return lambda c: ref[pl.ds(pl.multiple_of(c * mid, mid), mid), :]
-
-    halves(1, half_rows(scaled_t), emb)
     emb_acc[...] = emb.astype(F32)
-    step1(0)
 
     def grad_block(i):
         cut = pl.ds(pl.multiple_of(i * block, block), block)
-        scaled_grad = lax.dot_general(emb_acc[cut, :].astype(BF16), cp_v[...], NT, preferred_element_type=F32)
-        gained = scaled_grad * gain[...]
-        norm = normed[cut, :]
-        hidden_grad = inv_std[cut, 0:1] * (
-            gained
-            - jnp.mean(gained, axis=1, keepdims=True)
-            - norm * jnp.mean(gained * norm, axis=1, keepdims=True)
+        grad = emb_acc[cut, :]
+        first = jnp.sum(grad * flat, axis=1, keepdims=True)
+        second = jnp.sum(grad * blend[cut, :], axis=1, keepdims=True)
+        scaled_grad = lax.dot_general(grad.astype(BF16), cp_v[...], NT, preferred_element_type=F32)
+        hidden_grad = inv_std[cut, 0:1] * (scaled_grad * gain[...] - first - normed[cut, :] * second)
+        resid_grad[cut, :] = hidden_grad.astype(BF16)
+
+    loop(0, 4, grad_block)
+
+    mid = width // 2
+
+    def half_rows(ref, c):
+        return ref[pl.ds(pl.multiple_of(c * mid, mid), mid), :]
+
+    def proj_terms(c, name, group):
+        span = chunks // 2 * cw
+        term = jnp.dot(
+            half_rows(ctx_t, c), resid_grad[:, group * span : (group + 1) * span], preferred_element_type=F32
         )
-        resid_grad[cut, :] = hidden_grad.astype(BF16)
-
-    loop(0, 4, grad_block)
-
-    def context_block(i):
-        cut = pl.ds(i * block, block)
-        context_grad[cut, :] = lax.dot_general(
-            resid_grad[cut, :], wo_v[...], NT, preferred_element_type=F32
+        for k in range(chunks // 2):
+            ref = jobs[2 + group * (chunks // 2) + k][name]
+            ref[...] = term[:, k * cw : (k + 1) * cw].reshape(ref.shape).astype(ref.dtype)
+
+    def col_term(c, name):
+        ref = jobs[1][name]
+        term = jnp.dot(half_rows(scaled_t, c), emb_acc[...].astype(BF16), preferred_element_type=F32)
+        ref[...] = term.reshape(ref.shape).astype(ref.dtype)
+
+    for group in range(2):
+        proj_terms(other, "snd", group)
+        for k in range(chunks // 2):
+            pair_copy(2 + group * (chunks // 2) + k).start()
+    col_term(other, "snd")
+    pair_copy(1).start()
+    for group in range(2):
+        proj_terms(core, "own", group)
+    col_term(core, "own")
+
+    def query_terms():
+        def term(p):
+            j1, j2, rr = p // plane, lax.rem(p // nz, n2), lax.rem(p, nz)
+            s = at.slot(rr, j1, j2, other)
+            jobs[0]["snd"][p] = (u_all[s] * scale[pl.ds(s, 1), :]).astype(BF16)
+
+        loop(0, half, term)
+        pair_copy(0).start()
+
+    def below_terms(i):
+        def below(u):
+            for w in range(2):
+                s = u * 4 + w * 2
+                spread = jnp.concatenate([e_all[s], e_all[s + 1]], axis=1)
+                term = jnp.dot(flipped[...], spread, preferred_element_type=F32)
+                u_all[s] = term[:, :tok]
+                u_all[s + 1] = term[:, tok:]
+
+        loop(i * (n // 16), (i + 1) * (n // 16), below)
+
+    def context_terms(i):
+        cut = slice(i * (width // 4), (i + 1) * (width // 4))
+        context_grad[:, cut] = lax.dot_general(
+            resid_grad[...], wo_v[cut, :], NT, preferred_element_type=F32
         ).astype(BF16)
 
-    step1(1)
-    for k in range(chunks):
-        halves(2 + k, half_rows(ctx_t), resid_grad[:, k * cw : (k + 1) * cw])
-        if k > 0:
-            step1(1 + k)
-    context_block(0)
-    step1(1 + chunks)
+    def drain_gather():
+        each(nz, lambda k: z_copy(k).wait_send())
+        loop(0, half, lambda i: route(i, lambda copy: copy.wait_send()))
+        each(n, lambda k: msg_copy(k, me).wait_send())
+
+    fillers = [functools.partial(context_terms, i) for i in range(4)]
+    fillers += [functools.partial(below_terms, i) for i in range(4)] + [query_terms]
     steps = [None, step1, step2, step3, step4, step5, step6, step7, step8]
-    order = sorted((j + s, j, s) for j in range(1, chunks + 2) for s in range(2, 9))
-    late = chunks + 1
-    fillers = 1
-    for tick, j, s in order:
-        if j == 1 and fillers < 4:
-            context_block(fillers)
-            fillers += 1
-        if j == late and s == 4:
-            step2(0)
-        if j == late and s == 6:
-            step3(0)
-        if j == late and s == 7:
-            step4(0)
-        if j == late and s == 8:
-            each(n, lambda k: msg_copy(k, me).wait_send())
-            for k in range(chunks + 2):
-                drain_sum(k)
-            for k in range(1, chunks + 1):
-                drain_out(k)
-        steps[s](j)
-    drain_out(late)
+    for code in ORDER:
+        if code < 0:
+            if fillers:
+                fillers.pop(0)()
+            continue
+        if code == 1:
+            while fillers:
+                fillers.pop(0)()
+            drain_gather()
+        steps[code % 10](code // 10)
+    for j in range(chunks + 2):
+        drain_sum(j)
+    for j in range(1, chunks + 2):
+        drain_out(j)
 
 
 JOB = ("own", "snd", "pl", "b1", "k1", "l1", "b2", "l2", "b3", "k2", "l3")
@@ -572,7 +591,7 @@
     rows, width = residual.shape
     tok = own * per
     n = at.n
-    chunks = 4
+    chunks = 8
     cw = width // chunks
     piece = width // (2 * at.half)
     dma = pltpu.SemaphoreType.DMA
@@ -598,6 +617,7 @@
         vm((width, rows), BF16),
         vm((rows, width), F32),
         vm((rows, 128), F32),
+        vm((rows, dim), F32),
     ]
     scratch += job_buffers(at, dim, tok, own=False)
     scratch += job_buffers(at, piece, dim)

time: 83.7 us -> 75.7 us (0.904)
  Pallas kernels: 82.2 us -> 74.2 us
    pallas_call x1, Pallas kernels: 78.5 us -> 70.4 us  [body(): pl.pallas_call(functools.partial(main_kernel, dp, neg, own, per), out_sha...]
where the time goes in v3:
time: 75.7 us; the launch traced here: 75.5 us
  Pallas kernels  74.2 us (98%)
  between operations  1.32 us (2%)
    pallas_call x1, Pallas kernels, body(): pl.pallas_call(functools.partial(main_kernel, dp, neg, own, per), out_sha...  70.4 us
    pallas_call x1, Pallas kernels, body(): pl.pallas_call(finish_kernel, out_shape=[jax.ShapeDtypeStruct((width, wid...  3.75 us

profile of v3, /device:TPU:0, one launch (start us, length us, event | category | flops | bytes accessed | tf_op | source)
XLA Modules:
  0.0 75.5 jit_solution(6895568075733178623)
XLA Ops:
  1.3 0.0 copy-start
  1.3 0.0 copy-start.1
  1.3 70.4 %maxsim_main.1 = (f32[1,128]{1,0:T(1,128)S(1)}, f32[128,128]{1,0:T(8,128)S(1)}, bf16[512,1024]{1,0:T(8,128)(2,1)S(1)}, bf16[512,1024]{1,0:T(8,128)(2,1)S(1)}, bf...) custom-call(bf16[128,128]{1,0:T(8,128)(2,1)} %bitcast.13, s32[4]{0:T(128)} %positive_in.1, ...), custom_call_target="tpu_custom_call" | custom-call | tf_op jit(solution)/shard_map/maxsim_main/pallas_call | solution.py:641
  71.7 0.0 copy-done
  71.7 0.0 copy-done.1
  71.8 3.7 %maxsim_finish.1 = (f32[1024,1024]{1,0:T(8,128)}, f32[1024,128]{1,0:T(8,128)}, f32[1,1024]{1,0:T(1,128)}, f32[1,1]{1,0:T(1,128)}, f32[128,128]{1,0:T(8,128)}, /*...) custom-call(bf16[8,1024,128]{2,1,0:T(8,128)(2,1)S(1)} %bitcast.8, bf16[1024,128]{1,0:T(8,128)(2,1)S(1)} %bitcast.9, ...), custom_call_target="tpu_custom_call" | custom-call | tf_op jit(solution)/shard_map/maxsim_finish/pallas_call | solution.py:669
Async XLA Ops:
  1.3 70.5 %copy-start = (bf16[1024,128]{1,0:T(8,128)(2,1)S(1)}, bf16[1024,128]{1,0:T(8,128)(2,1)}, u32[]{:S(2)}) copy-start(bf16[1024,128]{1,0:T(8,128)(2,1)} %colbert.3) | copy-start | bytes 786436
  1.3 70.5 %copy-start.1 = (f32[1024]{0:T(1024)S(1)}, f32[1024]{0:T(1024)}, u32[]{:S(2)}) copy-start(f32[1024]{0:T(1024)} %param.16) | copy-start | bytes 12292

commit v4 on v3

--- a/solution.py
+++ b/solution.py
@@ -99,7 +99,7 @@
 
 
 def main_kernel(dp, neg, own, per, query, positive_in, passage, lengths, resid, context, out_proj, gain_in, colbert,
-                loss, query_grad, resid_grad, context_grad, sum_main, sum_col,
+                loss, query_grad, resid_grad, context_grad, summed,
                 q_all, msg, e_all, u_all, sums, inner, scale, bias, pas_v, flipped, emb_acc,
                 positive, gain, wo_v, cp_v, ctx_t, scaled_t, normed, inv_std, blend, *rest):
     at = Grid(dp, neg)
@@ -114,11 +114,11 @@
     wide = n * own
     rows, width = resid.shape
     block = rows // 4
-    chunks = sum_main.shape[0]
-    cw = sum_main.shape[-1]
+    chunks = summed.shape[0] - 1
+    cw = summed.shape[-1]
     count = len(JOB)
-    sems = rest[3 * count :]
-    ld, zs, a1s, a2s, pps, agr, xs, xr, rs_s, rs_r, ag_s, ag_r = sems
+    sems = rest[2 * count :]
+    ld, gs, agr, xs, xr, q_s, q_r, rs_s, rs_r, ag_s, ag_r = sems
 
     def dev1(t):
         return (r, at.column(lax.rem(i1 + t, n1), i2, core))
@@ -149,42 +149,36 @@
         pltpu.make_async_copy(out_proj, wo_v, ld.at[3]),
         pltpu.make_async_copy(resid, resid_grad, ld.at[4]),
         pltpu.make_async_copy(colbert, cp_v, ld.at[5]),
-        pltpu.make_async_copy(gain_in, gain, ld.at[7]),
-        pltpu.make_async_copy(positive_in, positive, ld.at[8]),
+        pltpu.make_async_copy(gain_in, gain, ld.at[6]),
+        pltpu.make_async_copy(positive_in, positive, ld.at[7]),
     ]
     for copy in loads:
         copy.start()
     loads[0].wait()
     pl.semaphore_wait(barrier, nz + n1 + n2 - 2)
 
-    def z_copy(k):
-        return remote(q_all.at[me], q_all.at[me], zs.at[k], agr.at[me], devz(k))
-
-    def a1_copy(s, rr, t):
-        return remote(q_all.at[s], q_all.at[s], a1s.at[rr, t], agr.at[s], dev1(t))
-
-    def a2_copy(s, rr, j1, t):
-        return remote(q_all.at[s], q_all.at[s], a2s.at[rr * n1 + j1, t], agr.at[s], dev2(t))
-
-    def pp_copy(s, rr, j1, j2):
-        return remote(q_all.at[s], q_all.at[s], pps.at[(j1 * n2 + j2) * nz + rr], agr.at[s], partner)
+    def arrived(ref, sem):
+        pltpu.make_async_copy(ref, ref, sem).wait()
+
+    def spread(s, device):
+        return remote(q_all.at[s], q_all.at[s], gs, agr.at[s], device)
 
     def landed(s):
-        remote(q_all.at[s], q_all.at[s], zs.at[0], agr.at[s], partner).wait_recv()
-
-    def route(i, act):
+        spread(s, partner).wait_recv()
+
+    def pass_on(i):
         rr, j1, j2 = at.arrival(i, core)
         s = at.slot(rr, j1, j2, core)
 
         @pl.when(i < nz)
         def _():
-            each(n1, lambda t: act(a1_copy(s, rr, t)))
+            each(n1, lambda t: spread(s, dev1(t)).start())
 
         @pl.when(i < nz * n1)
         def _():
-            each(n2, lambda t: act(a2_copy(s, rr, j1, t)))
-
-        act(pp_copy(s, rr, j1, j2))
+            each(n2, lambda t: spread(s, dev2(t)).start())
+
+        spread(s, partner).start()
 
     def attend(v):
         u, side = v // 2, lax.rem(v, 2)
@@ -209,8 +203,8 @@
             sums[pl.ds(s, 1), :] = total[:, cut]
             inner[pl.ds(s, 1), :] = level[:, cut]
 
-    each(nz, lambda k: z_copy(k).start())
-    route(0, lambda copy: copy.start())
+    each(nz, lambda k: spread(me, devz(k)).start())
+    pass_on(0)
     loads[1].wait()
     length = lengths[0]
     position = lax.broadcasted_iota(jnp.int32, bias.shape, 0)
@@ -219,7 +213,7 @@
 
     def relay(i):
         landed(at.slot(*at.arrival(i, core), core))
-        route(i, lambda copy: copy.start())
+        pass_on(i)
 
     def relay_step(i):
         relay(i)
@@ -248,10 +242,7 @@
     msg[me, :, :wide] = similar - shift
     msg[me, :, wide:] = chosen.astype(F32)
 
-    def msg_copy(k, slot):
-        return remote(msg.at[slot], msg.at[slot], xs.at[k], xr.at[k], any_device(k))
-
-    each(n, lambda k: msg_copy(k, me).start())
+    each(n, lambda k: remote(msg.at[me], msg.at[me], xs, xr, any_device(k)).start())
 
     for copy in loads[2:7]:
         copy.wait()
@@ -274,7 +265,7 @@
     loop(0, 4, norm_block)
     flat = exact(jnp.broadcast_to(gain[...], (8, width)), cp_v[...].astype(F32))[0:1, :] / width
 
-    each(n, lambda k: msg_copy(k, lax.rem(me - k + n, n)).wait_recv())
+    arrived(msg.at[pl.ds(1, n - 1)], xr)
 
     everyone = msg[:, :, :wide]
     picked = jnp.sum(msg[:, :, wide:], axis=0)
@@ -289,41 +280,35 @@
     laid = jnp.where(mine, jnp.broadcast_to(coefficient, mine.shape), 0.0)
     scale[...] = exact(laid, spots, NT) / sums[...]
 
-    jobs = []
-    for which_job, out in ((0, None), (1, sum_col)):
-        jobs.append(dict(zip(JOB, rest[which_job * count : (which_job + 1) * count]), out=out))
-    for k in range(chunks):
-        jobs.append(dict(zip(JOB, [ref.at[k] for ref in rest[2 * count : 3 * count]]), out=sum_main.at[k]))
+    jobs = [dict(zip(JOB, rest[:count]), out=None, sums=[(q_s.at[k], q_r.at[k]) for k in range(4)])]
+    stacked = dict(zip(JOB, rest[count : 2 * count]))
+    for j in range(1, chunks + 2):
+        k = chunks if j == 1 else j - 2
+        job = {name: ref.at[k] for name, ref in stacked.items()}
+        job["out"] = summed.at[k]
+        job["sums"] = [(rs_s.at[m], rs_r.at[k, m]) for m in range(4)]
+        job["outs"] = [(ag_s.at[m], ag_r.at[k, m]) for m in range(4)]
+        jobs.append(job)
 
     def pair_copy(j):
-        return remote(jobs[j]["snd"], jobs[j]["pl"], rs_s.at[j, 0, 0], rs_r.at[j, 0, 0], partner)
+        return remote(jobs[j]["snd"], jobs[j]["pl"], *jobs[j]["sums"][0], partner)
 
     def rs1_copy(j, t):
         there = pl.ds(lax.rem(i1 + t, n1) * plane, plane)
-        return remote(jobs[j]["b1"].at[there], jobs[j]["l1"].at[t], rs_s.at[j, 1, t], rs_r.at[j, 1, t], dev1(t))
+        return remote(jobs[j]["b1"].at[there], jobs[j]["l1"].at[t], *jobs[j]["sums"][1], dev1(t))
 
     def rs2_copy(j, t):
         there = pl.ds(lax.rem(i2 + t, n2) * nz, nz)
-        return remote(jobs[j]["b2"].at[there], jobs[j]["l2"].at[t], rs_s.at[j, 2, t], rs_r.at[j, 2, t], dev2(t))
+        return remote(jobs[j]["b2"].at[there], jobs[j]["l2"].at[t], *jobs[j]["sums"][2], dev2(t))
 
     def rs3_copy(j, k):
-        return remote(jobs[j]["b3"].at[lax.rem(r + k, nz)], jobs[j]["l3"].at[k], rs_s.at[j, 3, k], rs_r.at[j, 3, k], devz(k))
-
-    def ag3_copy(j, k, here):
-        piece = jobs[j]["out"].at[core, here]
-        return remote(piece, piece, ag_s.at[j, 0, k], ag_r.at[j, 0, k], devz(k))
-
-    def ag2_copy(j, t, j2):
-        piece = jobs[j]["out"].at[core, pl.ds((i1 * n2 + j2) * nz, nz)]
-        return remote(piece, piece, ag_s.at[j, 1, t], ag_r.at[j, 1, t], dev2(t))
-
-    def ag1_copy(j, t, j1):
-        piece = jobs[j]["out"].at[core, pl.ds(j1 * plane, plane)]
-        return remote(piece, piece, ag_s.at[j, 2, t], ag_r.at[j, 2, t], dev1(t))
-
-    def ag0_copy(j, c):
-        piece = jobs[j]["out"].at[c]
-        return remote(piece, piece, ag_s.at[j, 3, 0], ag_r.at[j, 3, 0], partner)
+        return remote(jobs[j]["b3"].at[lax.rem(r + k, nz)], jobs[j]["l3"].at[k], *jobs[j]["sums"][3], devz(k))
+
+    def out_copy(j, level, piece, device):
+        return remote(piece, piece, *jobs[j]["outs"][level], device)
+
+    def others(j, name, size):
+        return jobs[j][name].at[pl.ds(1, size - 1)]
 
     def step1(j):
         job = jobs[j]
@@ -353,9 +338,9 @@
 
     def step2(j):
         job = jobs[j]
+        arrived(others(j, "l1", n1), job["sums"][1][1])
         total = job["k1"][...]
         for t in range(1, n1):
-            rs1_copy(j, t).wait_recv()
             total = total + job["l1"][t].astype(F32)
         job["b2"][...] = total.astype(BF16)
         job["k1"][...] = total
@@ -364,9 +349,9 @@
 
     def step3(j):
         job = jobs[j]
+        arrived(others(j, "l2", n2), job["sums"][2][1])
         total = job["k1"][pl.ds(i2 * nz, nz)]
         for t in range(1, n2):
-            rs2_copy(j, t).wait_recv()
             total = total + job["l2"][t].astype(F32)
         job["b3"][...] = total.astype(BF16)
         job["k2"][...] = total
@@ -375,54 +360,35 @@
 
     def step4(j):
         job = jobs[j]
+        arrived(others(j, "l3", nz), job["sums"][3][1])
         total = job["k2"][r]
         for k in range(1, nz):
-            rs3_copy(j, k).wait_recv()
             total = total + job["l3"][k].astype(F32)
         if job["out"] is None:
             query_grad[...] = total.T
         else:
             job["out"][core, place] = total.astype(BF16)
             for k in range(1, nz):
-                ag3_copy(j, k, place).start()
+                out_copy(j, 0, job["out"].at[core, place], devz(k)).start()
 
     def step5(j):
-        for k in range(1, nz):
-            ag3_copy(j, k, (i1 * n2 + i2) * nz + lax.rem(r - k + nz, nz)).wait_recv()
+        arrived(others(j, "l3", nz), jobs[j]["outs"][0][1])
+        piece = jobs[j]["out"].at[core, pl.ds((i1 * n2 + i2) * nz, nz)]
         for t in range(1, n2):
-            ag2_copy(j, t, i2).start()
+            out_copy(j, 1, piece, dev2(t)).start()
 
     def step6(j):
-        for t in range(1, n2):
-            ag2_copy(j, t, lax.rem(i2 - t + n2, n2)).wait_recv()
+        arrived(others(j, "l2", n2), jobs[j]["outs"][1][1])
+        piece = jobs[j]["out"].at[core, pl.ds(i1 * plane, plane)]
         for t in range(1, n1):
-            ag1_copy(j, t, i1).start()
+            out_copy(j, 2, piece, dev1(t)).start()
 
     def step7(j):
-        for t in range(1, n1):
-            ag1_copy(j, t, lax.rem(i1 - t + n1, n1)).wait_recv()
-        ag0_copy(j, core).start()
+        arrived(others(j, "l1", n1), jobs[j]["outs"][2][1])
+        out_copy(j, 3, jobs[j]["out"].at[core], partner).start()
 
     def step8(j):
-        ag0_copy(j, other).wait_recv()
-
-    def drain_sum(j):
-        pair_copy(j).wait_send()
-        for t in range(1, n1):
-            rs1_copy(j, t).wait_send()
-        for t in range(1, n2):
-            rs2_copy(j, t).wait_send()
-        for k in range(1, nz):
-            rs3_copy(j, k).wait_send()
-
-    def drain_out(j):
-        for k in range(1, nz):
-            ag3_copy(j, k, place).wait_send()
-        for t in range(1, n2):
-            ag2_copy(j, t, i2).wait_send()
-        for t in range(1, n1):
-            ag1_copy(j, t, i1).wait_send()
-        ag0_copy(j, core).wait_send()
+        arrived(jobs[j]["pl"], jobs[j]["outs"][3][1])
 
     emb_acc[...] = jnp.zeros_like(emb_acc)
 
@@ -506,11 +472,6 @@
         context_grad[:, cut] = lax.dot_general(
             resid_grad[...], wo_v[cut, :], NT, preferred_element_type=F32
         ).astype(BF16)
-
-    def drain_gather():
-        each(nz, lambda k: z_copy(k).wait_send())
-        loop(0, half, lambda i: route(i, lambda copy: copy.wait_send()))
-        each(n, lambda k: msg_copy(k, me).wait_send())
 
     fillers = [functools.partial(context_terms, i) for i in range(4)]
     fillers += [functools.partial(below_terms, i) for i in range(4)] + [query_terms]
@@ -523,18 +484,25 @@
         if code == 1:
             while fillers:
                 fillers.pop(0)()
-            drain_gather()
         steps[code % 10](code // 10)
-    for j in range(chunks + 2):
-        drain_sum(j)
-    for j in range(1, chunks + 2):
-        drain_out(j)
+
+    arrived(q_all.at[pl.ds(1, n - 1)], gs)
+    arrived(msg.at[pl.ds(1, n - 1)], xs)
+    whole, first, second, third = stacked["pl"], stacked["l1"], stacked["l2"], stacked["l3"]
+    first = first.at[:, pl.ds(1, n1 - 1)]
+    second = second.at[:, pl.ds(1, n2 - 1)]
+    third = third.at[:, pl.ds(1, nz - 1)]
+    for sem, refs in ((rs_s, (whole, first, second, third)), (ag_s, (third, second, first, whole))):
+        for m, ref in enumerate(refs):
+            arrived(ref, sem.at[m])
+    for m, ref in enumerate((jobs[0]["pl"], others(0, "l1", n1), others(0, "l2", n2), others(0, "l3", nz))):
+        arrived(ref, q_s.at[m])
 
 
 JOB = ("own", "snd", "pl", "b1", "k1", "l1", "b2", "l2", "b3", "k2", "l3")
 
 
-def finish_kernel(main, col, gain, colbert, loss_in, query_in, resid_in, context_in,
+def finish_kernel(main, gain, colbert, loss_in, query_in, resid_in, context_in,
                   proj_grad, colbert_grad, gain_grad, loss, query_grad, resid_grad, context_grad, proj_v, sem):
     copies = [
         pltpu.make_async_copy(resid_in, resid_grad, sem.at[0]),
@@ -544,6 +512,7 @@
     for copy in copies:
         copy.start()
     chunks, rows, cw = main.shape
+    chunks = chunks - 1
     band = rows // 4
     for b in range(4):
         cut = slice(b * band, (b + 1) * band)
@@ -552,7 +521,7 @@
         copy = pltpu.make_async_copy(proj_v.at[cut], proj_grad.at[cut], sem.at[3 + b])
         copy.start()
         copies.append(copy)
-    wide = col[...].astype(F32)
+    wide = main[chunks].astype(F32)
     colbert_grad[...] = wide
     ones = jnp.ones((8, wide.shape[1]), F32)
     summed = exact(ones, wide * colbert[...].astype(F32), NT)
@@ -591,12 +560,11 @@
     rows, width = residual.shape
     tok = own * per
     n = at.n
-    chunks = 8
-    cw = width // chunks
+    chunks = width // dim
+    cw = dim
     piece = width // (2 * at.half)
     dma = pltpu.SemaphoreType.DMA
     vm = pltpu.VMEM
-    most = max(at.n1, at.n2, at.nz)
     scratch = [
         vm((n, tok, dim), BF16),
         vm((n, 1, 2 * n * own), F32),
@@ -620,36 +588,33 @@
         vm((rows, dim), F32),
     ]
     scratch += job_buffers(at, dim, tok, own=False)
-    scratch += job_buffers(at, piece, dim)
-    scratch += job_buffers(at, piece, cw, (chunks,))
+    scratch += job_buffers(at, piece, cw, (chunks + 1,))
     scratch += [
-        dma((9,)),
-        dma((at.nz,)),
-        dma((at.nz, at.n1)),
-        dma((at.nz * at.n1, at.n2)),
-        dma((at.half,)),
+        dma((8,)),
+        dma,
         dma((n,)),
-        dma((n,)),
-        dma((n,)),
-        dma((chunks + 2, 4, most)),
-        dma((chunks + 2, 4, most)),
-        dma((chunks + 2, 4, most)),
-        dma((chunks + 2, 4, most)),
+        dma,
+        dma,
+        dma((4,)),
+        dma((4,)),
+        dma((4,)),
+        dma((chunks + 1, 4)),
+        dma((4,)),
+        dma((chunks + 1, 4)),
     ]
-    held = sum(math.prod(ref.shape) * jnp.dtype(ref.dtype).itemsize for ref in scratch[:-12])
+    held = sum(math.prod(ref.shape) * jnp.dtype(ref.dtype).itemsize for ref in scratch[:-11])
     limit = min(held + held // 8 + 8 * 1024 * 1024, 67043328)
-    loss, query_grad, resid_grad, context_grad, sum_main, sum_col = pl.pallas_call(
+    loss, query_grad, resid_grad, context_grad, summed = pl.pallas_call(
         functools.partial(main_kernel, dp, neg, own, per),
         out_shape=[
             jax.ShapeDtypeStruct((1, 128), F32),
             jax.ShapeDtypeStruct((tok, dim), F32),
             jax.ShapeDtypeStruct((rows, width), BF16),
             jax.ShapeDtypeStruct((rows, width), BF16),
-            jax.ShapeDtypeStruct((chunks, 2, at.half, piece, cw), BF16),
-            jax.ShapeDtypeStruct((2, at.half, piece, dim), BF16),
+            jax.ShapeDtypeStruct((chunks + 1, 2, at.half, piece, cw), BF16),
         ],
         in_specs=[HBM, HBM, HBM, SMEM, HBM, HBM, HBM, HBM, HBM],
-        out_specs=[VMEM] * 6,
+        out_specs=[VMEM] * 5,
         scratch_shapes=scratch,
         compiler_params=pltpu.CompilerParams(
             collective_id=1, has_side_effects=True, vmem_limit_bytes=limit
@@ -677,14 +642,13 @@
             jax.ShapeDtypeStruct((rows, width), BF16),
             jax.ShapeDtypeStruct((rows, width), BF16),
         ],
-        in_specs=[VMEM] * 8,
+        in_specs=[VMEM] * 7,
         out_specs=[ANY, VMEM, VMEM, VMEM, ANY, ANY, ANY],
         scratch_shapes=[vm((width, width), F32), dma((7,))],
         compiler_params=pltpu.CompilerParams(vmem_limit_bytes=20000000),
         name="maxsim_finish",
     )(
-        sum_main.reshape(chunks, width, cw),
-        sum_col.reshape(width, dim),
+        summed.reshape(chunks + 1, width, cw),
         norm_gain[None, :],
         colbert_proj,
         loss,

time: 75.7 us -> 69.5 us (0.918)
  Pallas kernels: 74.2 us -> 68 us
    pallas_call x1, Pallas kernels: 70.4 us -> 64.2 us  [body(): pl.pallas_call(functools.partial(main_kernel, dp, neg, own, per), out_sha...]
where the time goes in v4:
time: 69.5 us; the launch traced here: 69.3 us
  Pallas kernels  68 us (98%)
  between operations  1.36 us (2%)
    pallas_call x1, Pallas kernels, body(): pl.pallas_call(functools.partial(main_kernel, dp, neg, own, per), out_sha...  64.2 us
    pallas_call x1, Pallas kernels, body(): pl.pallas_call(finish_kernel, out_shape=[jax.ShapeDtypeStruct((width, wid...  3.75 us

profile of v4, /device:TPU:0, one launch (start us, length us, event | category | flops | bytes accessed | tf_op | source)
XLA Modules:
  0.0 69.3 jit_solution(12197501544475721218)
XLA Ops:
  0.6 0.0 copy-start
  0.6 0.0 copy-start.1
  1.3 64.2 %maxsim_main.1 = (f32[1,128]{1,0:T(1,128)S(1)}, f32[128,128]{1,0:T(8,128)S(1)}, bf16[512,1024]{1,0:T(8,128)(2,1)S(1)}, bf16[512,1024]{1,0:T(8,128)(2,1)S(1)}, bf16[9,2,16,32,128]{4,3,2,1,0:T(8,128)(2,1)S(1)}) custom-call(bf16[128,128]{1,0:T(8,128)(2,1)} %bitcast.11, s32[4]{0:T(128)} %positive_in.1, bf16[512,128]{1,0:T(8,128)(2,1)} %bitcast.10, ...), custom_call_target="tpu_custom_call" | custom-call | tf_op jit(solution)/shard_map/maxsim_main/pallas_call | solution.py:607
  65.6 0.0 copy-done
  65.6 0.0 copy-done.1
  65.6 3.7 %maxsim_finish.1 = (f32[1024,1024]{1,0:T(8,128)}, f32[1024,128]{1,0:T(8,128)}, f32[1,1024]{1,0:T(1,128)}, f32[1,1]{1,0:T(1,128)}, f32[128,128]{1,0:T(8,128)}, /*...) custom-call(bf16[9,1024,128]{2,1,0:T(8,128)(2,1)S(1)} %bitcast.7, f32[1,1024]{1,0:T(1,128)S(1)} %bitcast.9, ...), custom_call_target="tpu_custom_call" | custom-call | tf_op jit(solution)/shard_map/maxsim_finish/pallas_call | solution.py:634
Async XLA Ops:
  0.6 64.9 %copy-start = (bf16[1024,128]{1,0:T(8,128)(2,1)S(1)}, bf16[1024,128]{1,0:T(8,128)(2,1)}, u32[]{:S(2)}) copy-start(bf16[1024,128]{1,0:T(8,128)(2,1)} %colbert.3) | copy-start | bytes 786436
  0.6 64.9 %copy-start.1 = (f32[1024]{0:T(1024)S(1)}, f32[1024]{0:T(1024)}, u32[]{:S(2)}) copy-start(f32[1024]{0:T(1024)} %param.16) | copy-start | bytes 12292

commit v5 on v4

--- a/solution.py
+++ b/solution.py
@@ -18,10 +18,13 @@
 BF16 = jnp.bfloat16
 NT = (((1,), (1,)), ((), ()))
 LAG = 2
+EARLY = 2
+TURNED = (2, 4, 7, 8)
 ORDER = (
-    21, -1, 41, -1, 51, -1, -1, -1, 91, -1, 22, -1, 42, 61, -1, 52, 71, -1, 92, 23, 81, 62, 31, 11, 43, 53, 72, 93, 63,
-    24, 82, 44, 32, 1, 73, 54, 94, 83, 33, 12, 25, 45, 74, 55, 2, 13, 46, 64, 84, 95, 34, 56, 14, 75, 26, 3, 65, 96, 85,
-    76, 35, 15, 66, 57, 97, 86, 36, 47, 16, 48, 77, 27, 67, 87, 58, 37, 17, 78, 98, 88, 28, 4, 68, 38, 18,
+    31, 21, -1, 51, 71, -1, -1, 32, 61, 41, -1, 22, -1, -1, 72, 91, -1, -1, 33, 52, 81, 11, -1, 23, 42, 62, 73, 53,
+    34, 92, 24, 12, 82, 43, 1, 63, 93, 13, 83, 44, 25, 64, 35, 74, 2, 26, 94, 54, 14, 45, 84, 36, 65, 75, 46, 3,
+    95, 55, 66, 15, 76, 85, 96, 56, 67, 16, 37, 4, 47, 27, 86, 97, 77, 38, 57, 68, 48, 17, 28, 78, 87, 58, 18, 98,
+    88,
 )
 
 
@@ -70,15 +73,15 @@
         self.y, self.x = g // self.b, lax.rem(g, self.b)
         self.me = self.r * self.neg + self.col
 
-    def flip(self, core):
-        return core if self.turned else 0 * core
-
-    def own(self, core):
-        f = self.flip(core)
+    def flip(self, core, turn=0):
+        return core * (1 - turn) + (1 - core) * turn if self.turned else 0 * core
+
+    def own(self, core, turn=0):
+        f = self.flip(core, turn)
         return (self.x * (1 - f) + self.y * f, self.y * (1 - f) + self.x * f)
 
-    def column(self, j1, j2, core):
-        f = self.flip(core)
+    def column(self, j1, j2, core, turn=0):
+        f = self.flip(core, turn)
         x, y = j1 * (1 - f) + j2 * f, j2 * (1 - f) + j1 * f
         return (y * self.b + x) * 2 + core
 
@@ -99,7 +102,7 @@
 
 
 def main_kernel(dp, neg, own, per, query, positive_in, passage, lengths, resid, context, out_proj, gain_in, colbert,
-                loss, query_grad, resid_grad, context_grad, summed,
+                loss, query_grad, resid_grad, context_grad, summed, summed_map,
                 q_all, msg, e_all, u_all, sums, inner, scale, bias, pas_v, flipped, emb_acc,
                 positive, gain, wo_v, cp_v, ctx_t, scaled_t, normed, inv_std, blend, *rest):
     at = Grid(dp, neg)
@@ -108,17 +111,17 @@
     other = 1 - core
     i1, i2 = at.own(core)
     n, n1, n2, nz, half, plane = at.n, at.n1, at.n2, at.nz, at.half, at.plane
-    place = (i1 * n2 + i2) * nz + r
     partner = (r, at.col + 1 - 2 * core)
+    away = 2 * (2 * r // nz) - 1
     tok = own * per
     wide = n * own
     rows, width = resid.shape
     block = rows // 4
-    chunks = summed.shape[0] - 1
+    chunks = summed.shape[0]
     cw = summed.shape[-1]
     count = len(JOB)
-    sems = rest[2 * count :]
-    ld, gs, agr, xs, xr, q_s, q_r, rs_s, rs_r, ag_s, ag_r = sems
+    sems = rest[3 * count :]
+    ld, gs, agr, xs, xr, q_s, q_r, c_s, c_r, rs_s, rs_r, ag_s, ag_r, ap_r = sems
 
     def dev1(t):
         return (r, at.column(lax.rem(i1 + t, n1), i2, core))
@@ -130,7 +133,7 @@
         return (lax.rem(r + k, nz), at.col)
 
     def any_device(k):
-        d = lax.rem(me + k, n)
+        d = lax.rem(me + k * away + n, n)
         return (d // neg, lax.rem(d, neg))
 
     barrier = pltpu.get_barrier_semaphore()
@@ -211,6 +214,25 @@
     bias[...] = jnp.where(position < length, 0.0, LOW)
     flipped[...] = pas_v[...].astype(F32).T.astype(BF16)
 
+    def norm_block(i):
+        cut = pl.ds(pl.multiple_of(i * block, block), block)
+        ctx = context_grad[cut, :]
+        hidden = resid_grad[cut, :].astype(F32) + jnp.dot(ctx, wo_v[...], preferred_element_type=F32)
+        centred = hidden - jnp.mean(hidden, axis=1, keepdims=True)
+        variance = jnp.mean(centred * centred, axis=1, keepdims=True)
+        inv = 1.0 / jnp.sqrt(variance + 1e-05)
+        norm = centred * inv
+        normed[cut, :] = norm
+        inv_std[cut, :] = jnp.broadcast_to(inv, (block, inv_std.shape[1]))
+        scaled = norm * gain[...]
+        scaled_t[:, cut] = scaled.T.astype(BF16)
+        blend[cut, :] = jnp.dot(scaled.astype(BF16), cp_v[...], preferred_element_type=F32) / width
+        ctx_t[:, cut] = ctx.astype(F32).T.astype(BF16)
+
+    for copy in loads[2:7]:
+        copy.wait()
+    loop(0, EARLY, norm_block)
+
     def relay(i):
         landed(at.slot(*at.arrival(i, core), core))
         pass_on(i)
@@ -244,25 +266,7 @@
 
     each(n, lambda k: remote(msg.at[me], msg.at[me], xs, xr, any_device(k)).start())
 
-    for copy in loads[2:7]:
-        copy.wait()
-
-    def norm_block(i):
-        cut = pl.ds(pl.multiple_of(i * block, block), block)
-        ctx = context_grad[cut, :]
-        hidden = resid_grad[cut, :].astype(F32) + jnp.dot(ctx, wo_v[...], preferred_element_type=F32)
-        centred = hidden - jnp.mean(hidden, axis=1, keepdims=True)
-        variance = jnp.mean(centred * centred, axis=1, keepdims=True)
-        inv = 1.0 / jnp.sqrt(variance + 1e-05)
-        norm = centred * inv
-        normed[cut, :] = norm
-        inv_std[cut, :] = jnp.broadcast_to(inv, (block, inv_std.shape[1]))
-        scaled = norm * gain[...]
-        scaled_t[:, cut] = scaled.T.astype(BF16)
-        blend[cut, :] = jnp.dot(scaled.astype(BF16), cp_v[...], preferred_element_type=F32) / width
-        ctx_t[:, cut] = ctx.astype(F32).T.astype(BF16)
-
-    loop(0, 4, norm_block)
+    loop(EARLY, 4, norm_block)
     flat = exact(jnp.broadcast_to(gain[...], (8, width)), cp_v[...].astype(F32))[0:1, :] / width
 
     arrived(msg.at[pl.ds(1, n - 1)], xr)
@@ -281,25 +285,40 @@
     scale[...] = exact(laid, spots, NT) / sums[...]
 
     jobs = [dict(zip(JOB, rest[:count]), out=None, sums=[(q_s.at[k], q_r.at[k]) for k in range(4)])]
-    stacked = dict(zip(JOB, rest[count : 2 * count]))
-    for j in range(1, chunks + 2):
-        k = chunks if j == 1 else j - 2
+    jobs.append(dict(zip(JOB, rest[count : 2 * count]), out=summed_map))
+    jobs[1]["sums"] = [(c_s.at[m], c_r.at[m]) for m in range(4)]
+    jobs[1]["outs"] = [(c_s.at[4 + m], c_r.at[4 + m]) for m in range(4)]
+    stacked = dict(zip(JOB, rest[2 * count : 3 * count]))
+    for k in range(chunks):
         job = {name: ref.at[k] for name, ref in stacked.items()}
-        job["out"] = summed.at[k]
+        job["out"] = summed.at[k, core]
         job["sums"] = [(rs_s.at[m], rs_r.at[k, m]) for m in range(4)]
-        job["outs"] = [(ag_s.at[m], ag_r.at[k, m]) for m in range(4)]
+        job["outs"] = [(ag_s.at[m], ag_r.at[k, m]) for m in range(3)] + [(ag_s.at[3], ap_r)]
         jobs.append(job)
+    for j, job in enumerate(jobs):
+        turn = 1 if j in TURNED else 0
+        job["at"] = h1, h2 = at.own(core, turn)
+        job["place"] = (h1 * n2 + h2) * nz + r
+        job["turn"] = turn
+
+    def job1(j, t):
+        h1, h2 = jobs[j]["at"]
+        return (r, at.column(lax.rem(h1 + t, n1), h2, core, jobs[j]["turn"]))
+
+    def job2(j, t):
+        h1, h2 = jobs[j]["at"]
+        return (r, at.column(h1, lax.rem(h2 + t, n2), core, jobs[j]["turn"]))
 
     def pair_copy(j):
         return remote(jobs[j]["snd"], jobs[j]["pl"], *jobs[j]["sums"][0], partner)
 
     def rs1_copy(j, t):
-        there = pl.ds(lax.rem(i1 + t, n1) * plane, plane)
-        return remote(jobs[j]["b1"].at[there], jobs[j]["l1"].at[t], *jobs[j]["sums"][1], dev1(t))
+        there = pl.ds(lax.rem(jobs[j]["at"][0] + t, n1) * plane, plane)
+        return remote(jobs[j]["b1"].at[there], jobs[j]["l1"].at[t], *jobs[j]["sums"][1], job1(j, t))
 
     def rs2_copy(j, t):
-        there = pl.ds(lax.rem(i2 + t, n2) * nz, nz)
-        return remote(jobs[j]["b2"].at[there], jobs[j]["l2"].at[t], *jobs[j]["sums"][2], dev2(t))
+        there = pl.ds(lax.rem(jobs[j]["at"][1] + t, n2) * nz, nz)
+        return remote(jobs[j]["b2"].at[there], jobs[j]["l2"].at[t], *jobs[j]["sums"][2], job2(j, t))
 
     def rs3_copy(j, k):
         return remote(jobs[j]["b3"].at[lax.rem(r + k, nz)], jobs[j]["l3"].at[k], *jobs[j]["sums"][3], devz(k))
@@ -315,7 +334,7 @@
         pair_copy(j).wait_recv()
         if j > 0:
             job["b1"][...] = (job["own"][...] + job["pl"][...].astype(F32)).astype(BF16)
-            kept = pl.ds(i1 * plane, plane)
+            kept = pl.ds(job["at"][0] * plane, plane)
             job["k1"][...] = job["own"][kept] + job["pl"][kept].astype(F32)
         else:
 
@@ -350,7 +369,7 @@
     def step3(j):
         job = jobs[j]
         arrived(others(j, "l2", n2), job["sums"][2][1])
-        total = job["k1"][pl.ds(i2 * nz, nz)]
+        total = job["k1"][pl.ds(job["at"][1] * nz, nz)]
         for t in range(1, n2):
             total = total + job["l2"][t].astype(F32)
         job["b3"][...] = total.astype(BF16)
@@ -367,28 +386,26 @@
         if job["out"] is None:
             query_grad[...] = total.T
         else:
-            job["out"][core, place] = total.astype(BF16)
+            job["out"][job["place"]] = total.astype(BF16)
             for k in range(1, nz):
-                out_copy(j, 0, job["out"].at[core, place], devz(k)).start()
+                out_copy(j, 0, job["out"].at[job["place"]], devz(k)).start()
 
     def step5(j):
         arrived(others(j, "l3", nz), jobs[j]["outs"][0][1])
-        piece = jobs[j]["out"].at[core, pl.ds((i1 * n2 + i2) * nz, nz)]
+        h1, h2 = jobs[j]["at"]
+        piece = jobs[j]["out"].at[pl.ds((h1 * n2 + h2) * nz, nz)]
         for t in range(1, n2):
-            out_copy(j, 1, piece, dev2(t)).start()
+            out_copy(j, 1, piece, job2(j, t)).start()
 
     def step6(j):
         arrived(others(j, "l2", n2), jobs[j]["outs"][1][1])
-        piece = jobs[j]["out"].at[core, pl.ds(i1 * plane, plane)]
+        piece = jobs[j]["out"].at[pl.ds(jobs[j]["at"][0] * plane, plane)]
         for t in range(1, n1):
-            out_copy(j, 2, piece, dev1(t)).start()
+            out_copy(j, 2, piece, job1(j, t)).start()
 
     def step7(j):
         arrived(others(j, "l1", n1), jobs[j]["outs"][2][1])
-        out_copy(j, 3, jobs[j]["out"].at[core], partner).start()
-
-    def step8(j):
-        arrived(jobs[j]["pl"], jobs[j]["outs"][3][1])
+        out_copy(j, 3, jobs[j]["out"], partner).start()
 
     emb_acc[...] = jnp.zeros_like(emb_acc)
 
@@ -432,20 +449,28 @@
             ref = jobs[2 + group * (chunks // 2) + k][name]
             ref[...] = term[:, k * cw : (k + 1) * cw].reshape(ref.shape).astype(ref.dtype)
 
-    def col_term(c, name):
+    def col_term(name):
         ref = jobs[1][name]
-        term = jnp.dot(half_rows(scaled_t, c), emb_acc[...].astype(BF16), preferred_element_type=F32)
+        term = jnp.dot(scaled_t[...], emb_acc[...].astype(BF16), preferred_element_type=F32)
         ref[...] = term.reshape(ref.shape).astype(ref.dtype)
 
     for group in range(2):
         proj_terms(other, "snd", group)
         for k in range(chunks // 2):
             pair_copy(2 + group * (chunks // 2) + k).start()
-    col_term(other, "snd")
-    pair_copy(1).start()
+
+    @pl.when(core == 0)
+    def _():
+        col_term("snd")
+        pair_copy(1).start()
+
     for group in range(2):
         proj_terms(core, "own", group)
-    col_term(core, "own")
+
+    @pl.when(core == 1)
+    def _():
+        col_term("own")
+
 
     def query_terms():
         def term(p):
@@ -475,7 +500,7 @@
 
     fillers = [functools.partial(context_terms, i) for i in range(4)]
     fillers += [functools.partial(below_terms, i) for i in range(4)] + [query_terms]
-    steps = [None, step1, step2, step3, step4, step5, step6, step7, step8]
+    steps = [None, step1, step2, step3, step4, step5, step6, step7]
     for code in ORDER:
         if code < 0:
             if fillers:
@@ -484,10 +509,28 @@
         if code == 1:
             while fillers:
                 fillers.pop(0)()
-        steps[code % 10](code // 10)
-
+        if code % 10 == len(steps):
+            continue
+        if code // 10 == 1:
+            pl.when(core == 1)(functools.partial(steps[code % 10], 1))
+        else:
+            steps[code % 10](code // 10)
+
+    arrived(stacked["pl"], ap_r)
     arrived(q_all.at[pl.ds(1, n - 1)], gs)
     arrived(msg.at[pl.ds(1, n - 1)], xs)
+
+    @pl.when(core == 0)
+    def _():
+        arrived(jobs[1]["pl"], c_s.at[0])
+        arrived(jobs[1]["pl"], c_r.at[7])
+
+    @pl.when(core == 1)
+    def _():
+        parts = [others(1, "l1", n1), others(1, "l2", n2), others(1, "l3", nz)]
+        for m, ref in enumerate(parts + parts[::-1] + [jobs[1]["pl"]]):
+            arrived(ref, c_s.at[1 + m])
+
     whole, first, second, third = stacked["pl"], stacked["l1"], stacked["l2"], stacked["l3"]
     first = first.at[:, pl.ds(1, n1 - 1)]
     second = second.at[:, pl.ds(1, n2 - 1)]
@@ -502,31 +545,33 @@
 JOB = ("own", "snd", "pl", "b1", "k1", "l1", "b2", "l2", "b3", "k2", "l3")
 
 
-def finish_kernel(main, gain, colbert, loss_in, query_in, resid_in, context_in,
-                  proj_grad, colbert_grad, gain_grad, loss, query_grad, resid_grad, context_grad, proj_v, sem):
-    copies = [
-        pltpu.make_async_copy(resid_in, resid_grad, sem.at[0]),
-        pltpu.make_async_copy(context_in, context_grad, sem.at[1]),
-        pltpu.make_async_copy(query_in, query_grad, sem.at[2]),
-    ]
-    for copy in copies:
+def finish_kernel(main, col, gain, colbert, loss_in, query_in, resid_in, context_in,
+                  proj_grad, colbert_grad, gain_grad, loss, query_grad, resid_grad, context_grad,
+                  proj_v, colbert_v, gain_v, sem):
+    copies = []
+
+    def send(src, dst):
+        copy = pltpu.make_async_copy(src, dst, sem.at[len(copies)])
         copy.start()
+        copies.append(copy)
+
+    send(resid_in, resid_grad)
+    send(context_in, context_grad)
+    send(query_in, query_grad)
+    loss[...] = loss_in[:, 0:1]
     chunks, rows, cw = main.shape
-    chunks = chunks - 1
+    wide = col[...].astype(F32)
+    colbert_v[...] = wide
+    send(colbert_v, colbert_grad)
     band = rows // 4
     for b in range(4):
         cut = slice(b * band, (b + 1) * band)
         for k in range(chunks):
             proj_v[cut, k * cw : (k + 1) * cw] = main[k, cut, :].astype(F32)
-        copy = pltpu.make_async_copy(proj_v.at[cut], proj_grad.at[cut], sem.at[3 + b])
-        copy.start()
-        copies.append(copy)
-    wide = main[chunks].astype(F32)
-    colbert_grad[...] = wide
+        send(proj_v.at[cut], proj_grad.at[cut])
     ones = jnp.ones((8, wide.shape[1]), F32)
-    summed = exact(ones, wide * colbert[...].astype(F32), NT)
-    gain_grad[...] = summed[0:1, :] / gain[...]
-    loss[...] = loss_in[:, 0:1]
+    gain_v[...] = exact(ones, wide * colbert[...].astype(F32), NT)[0:1, :] / gain[...]
+    send(gain_v, gain_grad)
     for copy in copies:
         copy.wait()
 
@@ -588,7 +633,8 @@
         vm((rows, dim), F32),
     ]
     scratch += job_buffers(at, dim, tok, own=False)
-    scratch += job_buffers(at, piece, cw, (chunks + 1,))
+    scratch += job_buffers(at, 2 * piece, cw)
+    scratch += job_buffers(at, piece, cw, (chunks,))
     scratch += [
         dma((8,)),
         dma,
@@ -597,24 +643,28 @@
         dma,
         dma((4,)),
         dma((4,)),
+        dma((8,)),
+        dma((8,)),
         dma((4,)),
-        dma((chunks + 1, 4)),
+        dma((chunks, 4)),
         dma((4,)),
-        dma((chunks + 1, 4)),
+        dma((chunks, 3)),
+        dma,
     ]
-    held = sum(math.prod(ref.shape) * jnp.dtype(ref.dtype).itemsize for ref in scratch[:-11])
+    held = sum(math.prod(ref.shape) * jnp.dtype(ref.dtype).itemsize for ref in scratch[:-14])
     limit = min(held + held // 8 + 8 * 1024 * 1024, 67043328)
-    loss, query_grad, resid_grad, context_grad, summed = pl.pallas_call(
+    loss, query_grad, resid_grad, context_grad, summed, summed_map = pl.pallas_call(
         functools.partial(main_kernel, dp, neg, own, per),
         out_shape=[
             jax.ShapeDtypeStruct((1, 128), F32),
             jax.ShapeDtypeStruct((tok, dim), F32),
             jax.ShapeDtypeStruct((rows, width), BF16),
             jax.ShapeDtypeStruct((rows, width), BF16),
-            jax.ShapeDtypeStruct((chunks + 1, 2, at.half, piece, cw), BF16),
+            jax.ShapeDtypeStruct((chunks, 2, at.half, piece, cw), BF16),
+            jax.ShapeDtypeStruct((at.half, 2 * piece, cw), BF16),
         ],
         in_specs=[HBM, HBM, HBM, SMEM, HBM, HBM, HBM, HBM, HBM],
-        out_specs=[VMEM] * 5,
+        out_specs=[VMEM] * 6,
         scratch_shapes=scratch,
         compiler_params=pltpu.CompilerParams(
             collective_id=1, has_side_effects=True, vmem_limit_bytes=limit
@@ -642,13 +692,14 @@
             jax.ShapeDtypeStruct((rows, width), BF16),
             jax.ShapeDtypeStruct((rows, width), BF16),
         ],
-        in_specs=[VMEM] * 7,
-        out_specs=[ANY, VMEM, VMEM, VMEM, ANY, ANY, ANY],
-        scratch_shapes=[vm((width, width), F32), dma((7,))],
+        in_specs=[VMEM] * 8,
+        out_specs=[ANY, ANY, ANY, VMEM, ANY, ANY, ANY],
+        scratch_shapes=[vm((width, width), F32), vm((width, dim), F32), vm((1, width), F32), dma((10,))],
         compiler_params=pltpu.CompilerParams(vmem_limit_bytes=20000000),
         name="maxsim_finish",
     )(
-        summed.reshape(chunks + 1, width, cw),
+        summed.reshape(chunks, width, cw),
+        summed_map.reshape(width, dim),
         norm_gain[None, :],
         colbert_proj,
         loss,

time: 69.5 us -> 67 us (0.964)
  Pallas kernels: 68 us -> 65.5 us
    pallas_call x1, Pallas kernels: 64.2 us -> 61.8 us  [body(): pl.pallas_call(functools.partial(main_kernel, dp, neg, own, per), out_sha...]
where the time goes in v5:
time: 67 us; the launch traced here: 66.8 us
  Pallas kernels  65.5 us (98%)
  between operations  1.32 us (2%)
    pallas_call x1, Pallas kernels, body(): pl.pallas_call(functools.partial(main_kernel, dp, neg, own, per), out_sha...  61.8 us
    pallas_call x1, Pallas kernels, body(): pl.pallas_call(finish_kernel, out_shape=[jax.ShapeDtypeStruct((width, wid...  3.66 us

profile of v5, /device:TPU:0, one launch (start us, length us, event | category | flops | bytes accessed | tf_op | source)
XLA Modules:
  0.0 66.8 jit_solution(6886637596116775058)
XLA Ops:
  1.3 0.0 copy-start
  1.3 0.0 copy-start.1
  1.3 61.8 %maxsim_main.1 = (f32[1,128]{1,0:T(1,128)S(1)}, f32[128,128]{1,0:T(8,128)S(1)}, bf16[512,1024]{1,0:T(8,128)(2,1)S(1)}, bf16[512,1024]{1,0:T(8,128)(2,1)S(1)}, bf...) custom-call(bf16[128,128]{1,0:T(8,128)(2,1)} %bitcast.13, s32[4]{0:T(128)} %positive_in.1, ...), custom_call_target="tpu_custom_call" | custom-call | tf_op jit(solution)/shard_map/maxsim_main/pallas_call | solution.py:656
  63.1 0.0 copy-done
  63.1 0.0 copy-done.1
  63.1 3.7 %maxsim_finish.1 = (f32[1024,1024]{1,0:T(8,128)}, f32[1024,128]{1,0:T(8,128)}, f32[1,1024]{1,0:T(1,128)}, f32[1,1]{1,0:T(1,128)}, f32[128,128]{1,0:T(8,128)}, /*...) custom-call(bf16[8,1024,128]{2,1,0:T(8,128)(2,1)S(1)} %bitcast.8, bf16[1024,128]{1,0:T(8,128)(2,1)S(1)} %bitcast.9, ...), custom_call_target="tpu_custom_call" | custom-call | tf_op jit(solution)/shard_map/maxsim_finish/pallas_call | solution.py:684
Async XLA Ops:
  1.3 61.8 %copy-start = (bf16[1024,128]{1,0:T(8,128)(2,1)S(1)}, bf16[1024,128]{1,0:T(8,128)(2,1)}, u32[]{:S(2)}) copy-start(bf16[1024,128]{1,0:T(8,128)(2,1)} %colbert.3) | copy-start | bytes 786436
  1.3 61.8 %copy-start.1 = (f32[1024]{0:T(1024)S(1)}, f32[1024]{0:T(1024)}, u32[]{:S(2)}) copy-start(f32[1024]{0:T(1024)} %param.16) | copy-start | bytes 12292

commit v6 on v5

--- a/solution.py
+++ b/solution.py
@@ -19,12 +19,12 @@
 NT = (((1,), (1,)), ((), ()))
 LAG = 2
 EARLY = 2
-TURNED = (2, 4, 7, 8)
+TURNED = ()
 ORDER = (
-    31, 21, -1, 51, 71, -1, -1, 32, 61, 41, -1, 22, -1, -1, 72, 91, -1, -1, 33, 52, 81, 11, -1, 23, 42, 62, 73, 53,
-    34, 92, 24, 12, 82, 43, 1, 63, 93, 13, 83, 44, 25, 64, 35, 74, 2, 26, 94, 54, 14, 45, 84, 36, 65, 75, 46, 3,
-    95, 55, 66, 15, 76, 85, 96, 56, 67, 16, 37, 4, 47, 27, 86, 97, 77, 38, 57, 68, 48, 17, 28, 78, 87, 58, 18, 98,
-    88,
+    21, 31, 41, 51, 61, -1, -1, -1, 22, 32, 71, -1, -1, 42, 81, -1, 62, 52, 91, 23, -1, -1, 33, -1, 43, 72, 11, 63,
+    82, 53, 24, 92, 73, 34, 12, 1, 83, 93, 64, 44, 25, 13, 54, 35, 2, 84, 94, 45, 65, 74, 36, 26, 14, 55, 85, 66,
+    46, 75, 95, 3, 56, 15, 86, 27, 76, 96, 47, 37, 57, 16, 67, 87, 28, 77, 4, 68, 38, 97, 88, 58, 78, 48, 17, 98,
+    18,
 )
 
 

time: 67 us -> 65.9 us (0.984)
  Pallas kernels: 65.5 us -> 64.4 us
    pallas_call x1, Pallas kernels: 61.8 us -> 60.7 us  [body(): pl.pallas_call(functools.partial(main_kernel, dp, neg, own, per), out_sha...]
where the time goes in v6:
time: 65.9 us; the launch traced here: 65.7 us
  Pallas kernels  64.4 us (98%)
  between operations  1.32 us (2%)
    pallas_call x1, Pallas kernels, body(): pl.pallas_call(functools.partial(main_kernel, dp, neg, own, per), out_sha...  60.7 us
    pallas_call x1, Pallas kernels, body(): pl.pallas_call(finish_kernel, out_shape=[jax.ShapeDtypeStruct((width, wid...  3.66 us

profile of v6, /device:TPU:0, one launch (start us, length us, event | category | flops | bytes accessed | tf_op | source)
XLA Modules:
  0.0 65.7 jit_solution(9963949815043546748)
XLA Ops:
  1.3 0.0 copy-start
  1.3 0.0 copy-start.1
  1.3 60.7 %maxsim_main.1 = (f32[1,128]{1,0:T(1,128)S(1)}, f32[128,128]{1,0:T(8,128)S(1)}, bf16[512,1024]{1,0:T(8,128)(2,1)S(1)}, bf16[512,1024]{1,0:T(8,128)(2,1)S(1)}, bf...) custom-call(bf16[128,128]{1,0:T(8,128)(2,1)} %bitcast.13, s32[4]{0:T(128)} %positive_in.1, ...), custom_call_target="tpu_custom_call" | custom-call | tf_op jit(solution)/shard_map/maxsim_main/pallas_call | solution.py:656
  62.0 0.0 copy-done
  62.0 0.0 copy-done.1
  62.1 3.7 %maxsim_finish.1 = (f32[1024,1024]{1,0:T(8,128)}, f32[1024,128]{1,0:T(8,128)}, f32[1,1024]{1,0:T(1,128)}, f32[1,1]{1,0:T(1,128)}, f32[128,128]{1,0:T(8,128)}, /*...) custom-call(bf16[8,1024,128]{2,1,0:T(8,128)(2,1)S(1)} %bitcast.8, bf16[1024,128]{1,0:T(8,128)(2,1)S(1)} %bitcast.9, ...), custom_call_target="tpu_custom_call" | custom-call | tf_op jit(solution)/shard_map/maxsim_finish/pallas_call | solution.py:684
Async XLA Ops:
  1.3 60.8 %copy-start = (bf16[1024,128]{1,0:T(8,128)(2,1)S(1)}, bf16[1024,128]{1,0:T(8,128)(2,1)}, u32[]{:S(2)}) copy-start(bf16[1024,128]{1,0:T(8,128)(2,1)} %colbert.3) | copy-start | bytes 786436
  1.3 60.8 %copy-start.1 = (f32[1024]{0:T(1024)S(1)}, f32[1024]{0:T(1024)}, u32[]{:S(2)}) copy-start(f32[1024]{0:T(1024)} %param.16) | copy-start | bytes 12292

commit v7 on v6

--- a/solution.py
+++ b/solution.py
@@ -565,13 +565,14 @@
     send(colbert_v, colbert_grad)
     band = rows // 4
     for b in range(4):
+        if b == 3:
+            ones = jnp.ones((8, wide.shape[1]), F32)
+            gain_v[...] = exact(ones, wide * colbert[...].astype(F32), NT)[0:1, :] / gain[...]
+            send(gain_v, gain_grad)
         cut = slice(b * band, (b + 1) * band)
         for k in range(chunks):
             proj_v[cut, k * cw : (k + 1) * cw] = main[k, cut, :].astype(F32)
         send(proj_v.at[cut], proj_grad.at[cut])
-    ones = jnp.ones((8, wide.shape[1]), F32)
-    gain_v[...] = exact(ones, wide * colbert[...].astype(F32), NT)[0:1, :] / gain[...]
-    send(gain_v, gain_grad)
     for copy in copies:
         copy.wait()
 

time: 65.9 us -> 65.9 us (level)
  no operation moved by 1% of the time
where the time goes in v7:
time: 65.9 us; the launch traced here: 65.7 us
  Pallas kernels  64.4 us (98%)
  between operations  1.32 us (2%)
    pallas_call x1, Pallas kernels, body(): pl.pallas_call(functools.partial(main_kernel, dp, neg, own, per), out_sha...  60.7 us
    pallas_call x1, Pallas kernels, body(): pl.pallas_call(finish_kernel, out_shape=[jax.ShapeDtypeStruct((width, wid...  3.66 us

profile of v7, /device:TPU:0, one launch (start us, length us, event | category | flops | bytes accessed | tf_op | source)
XLA Modules:
  0.0 65.7 jit_solution(6272093429360291298)
XLA Ops:
  1.3 0.0 copy-start
  1.3 0.0 copy-start.1
  1.3 60.7 %maxsim_main.1 = (f32[1,128]{1,0:T(1,128)S(1)}, f32[128,128]{1,0:T(8,128)S(1)}, bf16[512,1024]{1,0:T(8,128)(2,1)S(1)}, bf16[512,1024]{1,0:T(8,128)(2,1)S(1)}, bf...) custom-call(bf16[128,128]{1,0:T(8,128)(2,1)} %bitcast.13, s32[4]{0:T(128)} %positive_in.1, ...), custom_call_target="tpu_custom_call" | custom-call | tf_op jit(solution)/shard_map/maxsim_main/pallas_call | solution.py:657
  62.0 0.0 copy-done
  62.0 0.0 copy-done.1
  62.1 3.7 %maxsim_finish.1 = (f32[1024,1024]{1,0:T(8,128)}, f32[1024,128]{1,0:T(8,128)}, f32[1,1024]{1,0:T(1,128)}, f32[1,1]{1,0:T(1,128)}, f32[128,128]{1,0:T(8,128)}, /*...) custom-call(bf16[8,1024,128]{2,1,0:T(8,128)(2,1)S(1)} %bitcast.8, bf16[1024,128]{1,0:T(8,128)(2,1)S(1)} %bitcast.9, ...), custom_call_target="tpu_custom_call" | custom-call | tf_op jit(solution)/shard_map/maxsim_finish/pallas_call | solution.py:685
Async XLA Ops:
  1.3 60.8 %copy-start = (bf16[1024,128]{1,0:T(8,128)(2,1)S(1)}, bf16[1024,128]{1,0:T(8,128)(2,1)}, u32[]{:S(2)}) copy-start(bf16[1024,128]{1,0:T(8,128)(2,1)} %colbert.3) | copy-start | bytes 786436
  1.3 60.8 %copy-start.1 = (f32[1024]{0:T(1024)S(1)}, f32[1024]{0:T(1024)}, u32[]{:S(2)}) copy-start(f32[1024]{0:T(1024)} %param.16) | copy-start | bytes 12292
